TPU v7x, 8 devices: a whole 2x2x1 slice. The times are simulated.
8 devices in a mesh: rep: 1 (over z), dp: 8 (over x, y, core).
Axes of the slice: x: 2, y: 2, z: 1, core: 2. Of those that a mesh axis runs over, the one named last changes fastest.
Arguments:
- x: bfloat16 [8, 2048, 896], P(('rep', 'dp'))
- dy: bfloat16 [8, 2048, 896], P(('rep', 'dp'))
- w_gate: bfloat16 [2, 896, 2560], replicated
- w_up: bfloat16 [2, 896, 2560], replicated
- w_down: bfloat16 [2, 2560, 896], replicated
- m_w_gate: float32 [2, 896, 2560], P(None, 'dp')
- m_w_up: float32 [2, 896, 2560], P(None, 'dp')
- m_w_down: float32 [2, 2560, 896], P(None, 'dp')
- v_w_gate: float32 [2, 896, 2560], P(None, 'dp')
- v_w_up: float32 [2, 896, 2560], P(None, 'dp')
- v_w_down: float32 [2, 2560, 896], P(None, 'dp')
Outputs:
- output 1: bfloat16 [2, 896, 2560], P('rep')
- output 2: bfloat16 [2, 896, 2560], P('rep')
- output 3: bfloat16 [2, 2560, 896], P('rep')
- output 4: float32 [2, 896, 2560], P('rep', 'dp')
- output 5: float32 [2, 896, 2560], P('rep', 'dp')
- output 6: float32 [2, 2560, 896], P('rep', 'dp')
- output 7: float32 [2, 896, 2560], P('rep', 'dp')
- output 8: float32 [2, 896, 2560], P('rep', 'dp')
- output 9: float32 [2, 2560, 896], P('rep', 'dp')
All inputs are finite; a program needn't handle non-finite values.
Results may differ from a plain program's by a relative error of at most 0.022.
Values are sent between devices in bfloat16 or wider.
A program may use at most 2 GiB of HBM per device.

v0:
```python
import functools

import jax
import jax.numpy as jnp
from jax import lax
from jax.experimental import pallas as pl
from jax.experimental.pallas import tpu as pltpu
from jax.sharding import PartitionSpec as P


F32, BF = jnp.float32, jnp.bfloat16
VMEM = 67043328
X, Y, CORE = 4, 2, 1
PARTS = 2


def dot(a, b, ca=1, cb=0):
    return lax.dot_general(a, b, (((ca,), (cb,)), ((), ())), preferred_element_type=F32)


def norm_scale(wide):
    return lax.rsqrt(jnp.mean(wide * wide, -1, keepdims=True) + 1e-6)


def whole(shape):
    return pl.BlockSpec(shape, lambda i, *_: (0,) * len(shape), pipeline_mode=pl.Buffered(1))


def sds(shape, dtype):
    return jax.ShapeDtypeStruct(shape, dtype)


def params():
    return pltpu.CompilerParams(vmem_limit_bytes=VMEM)


def cost(matmuls, n, d, ff, bytes_accessed):
    return pl.CostEstimate(flops=2 * matmuls * n * d * ff, bytes_accessed=bytes_accessed, transcendentals=0)


def forward_kernel(chunk, down, h_ref, wg_ref, wu_ref, *refs):
    if down:
        wd_ref, a_ref, act_ref, sa_ref, sb_ref, h1_ref = refs
    else:
        a_ref, act_ref, sa_ref, sb_ref = refs
    wide = h_ref[...].astype(F32)
    a = (wide * norm_scale(wide)).astype(BF)
    a_ref[...] = a
    for c in range(wg_ref.shape[1] // chunk):
        s = pl.ds(c * chunk, chunk)
        gate, up = dot(a, wg_ref[:, s]), dot(a, wu_ref[:, s])
        sig = 1.0 / (1.0 + jnp.exp(-gate))
        silu = gate * sig
        act_ref[:, s] = (silu * up).astype(BF)
        sb_ref[:, s] = silu
        sa_ref[:, s] = up * (sig + silu * (1.0 - sig))
    if down:
        out = dot(act_ref[...], wd_ref[...]).astype(BF)
        h1_ref[...] = (h_ref[...].astype(F32) + out.astype(F32)).astype(BF)


def forward(number, h, weights, down, tile=256, chunk=1280):
    n, d = h.shape
    ff = weights[0].shape[2]
    row = lambda w: pl.BlockSpec((tile, w), lambda i: (i, 0))
    of = lambda w: pl.BlockSpec((None, *w.shape[1:]), lambda i: (number, 0, 0), pipeline_mode=pl.Buffered(1))
    used = weights[: 2 + down]
    return pl.pallas_call(
        functools.partial(forward_kernel, chunk, down),
        grid=(n // tile,),
        in_specs=[row(d)] + [of(w) for w in used],
        out_specs=[row(d), row(ff), row(ff), row(ff)] + [row(d)] * down,
        out_shape=[sds((n, d), BF), sds((n, ff), BF), sds((n, ff), F32), sds((n, ff), F32)] + [sds((n, d), BF)] * down,
        compiler_params=params(),
        cost_estimate=cost(3 if down else 2, n, d, ff, 10 * n * ff),
        name="forward",
    )(h, *used)


def peers():
    me = lax.axis_index("dp")
    x, y, core = me // 4, me // 2 % 2, me % 2
    return (x, y, core), (me + 1 - 2 * core, me + 2 - 4 * y, me + 4 - 8 * x)


def xor(a, b):
    return a + b - 2 * a * b


def send(src, dst, sems, to):
    return pltpu.make_async_remote_copy(
        src_ref=src,
        dst_ref=dst,
        send_sem=sems[0],
        recv_sem=sems[1],
        device_id={"dp": to},
        device_id_type=pl.DeviceIdType.MESH,
    )


def total(*terms):
    return sum(t.astype(F32) for t in terms)


def backward_kernel(states, tokens, tile, steps, *refs):
    refs = list(refs)
    take = lambda k: [refs.pop(0) for _ in range(k)]
    a_ref, dy_ref, act_ref, sa_ref, sb_ref, wd_ref = take(6)
    h_ref, wg_ref, wu_ref = take(3) if states else (None,) * 3
    (before_ref,) = (None,) if states else take(1)
    gate_ref, up_ref, down_ref = take(3)
    (squares_ref,) = take(1)
    (dh_ref,) = take(1) if states else (None,)
    dg_s, du_s = take(2)
    dk, do, di, da_sum, db_sum, dsx, dsy, drx, dry, dsy2, dsx2, dry2, drx2 = take(13)
    gk, go, gi, g_sum, gs1, gr1, gs2, gr2 = take(8)
    uk, uo, ui, u_sum, us1, ur1, us2, ur2 = take(8)
    d_core, d_link, p_core, p_link = take(4)
    if states:
        da_s, h_s, dh_s, h_sem, dh_sem = take(5)
    else:
        sq_s, sq_in, sq_sem = take(3)

    n, d = a_ref.shape
    parts = n // tokens
    i = pl.program_id(0)
    (x, y, core), (to_core, to_y, to_x) = peers()
    mine = core == 0

    def down_copy(q):
        sx, sy = xor(q // 2, x), xor(q % 2, y)
        return send(do.at[sx, sy], di.at[sx, sy], (d_core.at[0, q], d_core.at[1, q]), to_core)

    def down_links(stage):
        sem = lambda k: (d_link.at[0, k], d_link.at[1, k])
        if stage == 1:
            return send(dsx, drx, sem(0), to_x), send(dsy, dry, sem(1), to_y)
        return send(dsy2, dry2, sem(2), to_y), send(dsx2, drx2, sem(3), to_x)

    def core_copy(which, u):
        src, dst = ((go, gi), (uo, ui))[which]
        slot = u % 2
        return send(src, dst.at[slot], (p_core.at[0, which, slot], p_core.at[1, which, slot]), to_core)

    def pair_links(stage, u):
        sem = lambda k: (p_link.at[0, k, u], p_link.at[1, k, u])
        if stage == 1:
            return send(gs1, gr1.at[u], sem(0), to_x), send(us1, ur1.at[u], sem(1), to_y)
        return send(gs2.at[u % 2], gr2.at[u], sem(2), to_y), send(us2.at[u % 2], ur2.at[u], sem(3), to_x)

    def start(copies):
        for c in copies:
            c.start()

    def wait(copies):
        for c in copies:
            c.wait()

    def other(k):
        return 4 * xor(x, k // 4) + 2 * xor(y, k // 2 % 2) + xor(core, k % 2)

    def square_sum():
        return sum(jnp.sum(jnp.square(ref[...].astype(F32))) for ref in (gate_ref, up_ref, down_ref))

    half = dk.shape[2] // 2
    lo, hi = pl.ds(0, half), pl.ds(half, half)

    def down_first():
        wait([down_copy(q) for q in range(4)])
        dsx[...] = total(dk[1, :, lo], di[1, :, lo]).astype(BF)
        dsy[...] = total(dk[:, 1, hi], di[:, 1, hi]).astype(BF)
        start(down_links(1))
        da_sum[...] = total(dk[0, :, lo], di[0, :, lo])
        db_sum[...] = total(dk[:, 0, hi], di[:, 0, hi])

    def down_second():
        wait(down_links(1))
        dsy2[...] = total(da_sum[1], drx[1]).astype(BF)
        dsx2[...] = total(db_sum[1], dry[1]).astype(BF)
        start(down_links(2))
        da_sum[0] = total(da_sum[0], drx[0])
        db_sum[0] = total(db_sum[0], dry[0])

    def down_last():
        wait(down_links(2))
        down_ref[lo, :] = total(da_sum[0], dry2[...]).astype(BF)
        down_ref[hi, :] = total(db_sum[0], drx2[...]).astype(BF)

    def pair_first(u):
        slot = u % 2
        wait([core_copy(0, u), core_copy(1, u)])
        gs1[...] = total(gk[1], gi[slot, 1]).astype(BF)
        us1[...] = total(uk[:, 1], ui[slot, :, 1]).astype(BF)
        start(pair_links(1, u))
        g_sum[slot] = total(gk[0], gi[slot, 0])
        u_sum[slot] = total(uk[:, 0], ui[slot, :, 0])

    def pair_second(u):
        slot = u % 2
        wait(pair_links(1, u))
        gs2[slot] = total(g_sum[slot, 1], gr1[u, 1]).astype(BF)
        us2[slot] = total(u_sum[slot, 1], ur1[u, 1]).astype(BF)
        start(pair_links(2, u))
        g_sum[slot, 0] = total(g_sum[slot, 0], gr1[u, 0])
        u_sum[slot, 0] = total(u_sum[slot, 0], ur1[u, 0])

    def pair_last(u):
        slot = u % 2
        wait(pair_links(2, u))
        cols = pl.ds(pl.multiple_of(u * tile, tile), tile)
        gate_ref[:, cols] = total(g_sum[slot, 0], gr2[u]).astype(BF)
        up_ref[:, cols] = total(u_sum[slot, 0], ur2[u]).astype(BF)

    @pl.when(i == 0)
    def _():
        barrier = pltpu.get_barrier_semaphore()
        met = (to_core, to_y, to_x) if states else [other(k) for k in range(1, 8)]
        for to in met:
            pl.semaphore_signal(barrier, inc=1, device_id={"dp": to}, device_id_type=pl.DeviceIdType.MESH)
        pl.semaphore_wait(barrier, len(met))
        if states:

            def clear(t, _):
                da_s[pl.ds(pl.multiple_of(t * 256, 256), 256), :] = jnp.zeros((256, d), F32)
                return 0

            lax.fori_loop(0, n // 256, clear, 0)

    @pl.when(i < 4)
    def _():
        g = dot(act_ref[...], dy_ref[...], 0, 0)
        rows = g.shape[0] // 2
        sx, sy = xor(i // 2, x), xor(i % 2, y)
        dk[sx, sy] = jnp.where(mine, g[:rows], g[rows:]).astype(BF)
        do[sx, sy] = jnp.where(mine, g[rows:], g[:rows]).astype(BF)
        down_copy(i).start()

    @pl.when(i >= 4)
    def _():
        j, t = (i - 4) // parts, (i - 4) % parts
        r = pl.ds(pl.multiple_of(t * tokens, tokens), tokens)
        dp = dot(dy_ref[r, :], wd_ref[...], 1, 1).astype(BF).astype(F32)
        du = (dp * sb_ref[...]).astype(BF)
        dg = (dp * sa_ref[...]).astype(BF)
        dg_s[r, :], du_s[r, :] = dg, du
        if states:
            da_s[r, :] += dot(dg, wg_ref[...], 1, 1) + dot(du, wu_ref[...], 1, 1)

        @pl.when(t == parts - 1)
        def _():
            pl.when(j == 0)(down_first)
            pl.when(j == 2)(down_second)
            pl.when(j >= 2)(lambda: pair_second(j - 2))
            pl.when(j >= 3)(lambda: pair_last(j - 3))
            pl.when(j >= 1)(lambda: pair_first(j - 1))
            pl.when(j == 3)(down_last)
            rows = d // 8
            for which, (by, keep, out) in enumerate(((dg_s, gk, go), (du_s, uk, uo))):
                g = dot(a_ref[...], by[...], 0, 0)
                for q in range(4):
                    first, second = (g[(2 * q + e) * rows : (2 * q + e + 1) * rows] for e in (0, 1))
                    sx, sy = xor(q // 2, x), xor(q % 2, y)
                    keep[sx, sy] = jnp.where(mine, first, second).astype(BF)
                    out[sx, sy] = jnp.where(mine, second, first).astype(BF)
                core_copy(which, j).start()

    @pl.when(i == 4 + steps * parts - 1)
    def _():
        pair_second(steps - 2)
        pair_last(steps - 3)
        pair_first(steps - 1)
        if states:

            def fetch(t):
                rows = pl.ds(pl.multiple_of(t * 256, 256), 256)
                return pltpu.make_async_copy(h_ref.at[rows, :], h_s.at[t % 2], h_sem.at[t % 2])

            def store(t):
                rows = pl.ds(pl.multiple_of(t * 256, 256), 256)
                return pltpu.make_async_copy(dh_s.at[t % 2], dh_ref.at[rows, :], dh_sem.at[t % 2])

            fetch(0).start()

            def back(t, _):
                r = pl.ds(pl.multiple_of(t * 256, 256), 256)
                fetch(t).wait()
                pl.when(t + 1 < n // 256)(lambda: fetch(t + 1).start())
                da = da_s[r, :].astype(BF).astype(F32)
                wide = h_s[t % 2].astype(F32)
                s = norm_scale(wide)
                dx = s * (da - wide * (s * s * jnp.mean(da * wide, -1, keepdims=True)))
                pl.when(t >= 2)(lambda: store(t - 2).wait())
                dh_s[t % 2] = (dy_ref[r, :].astype(F32) + dx.astype(BF).astype(F32)).astype(BF)
                store(t).start()
                return 0

            lax.fori_loop(0, n // 256, back, 0)
            store(n // 256 - 2).wait()
            store(n // 256 - 1).wait()
        pair_second(steps - 1)
        pair_last(steps - 2)
        pair_last(steps - 1)
        if states:
            squares_ref[...] = jnp.full(squares_ref.shape, square_sum(), F32)
            return
        sq_s[...] = before_ref[...] + square_sum()
        copies = [send(sq_s, sq_in.at[k], (sq_sem.at[0, k], sq_sem.at[1, k]), other(k)) for k in range(1, 8)]
        start(copies)
        wait(copies)
        sq_in[0] = sq_s[...]
        parts_of = [sq_in[k] for k in range(8)]
        while len(parts_of) > 1:
            parts_of = [one + two for one, two in zip(parts_of[::2], parts_of[1::2], strict=True)]
        squares_ref[...] = parts_of[0]


def backward(number, a, dy, act, sa, sb, weights, h=None, before=None, tokens=512, tile=512):
    wg, wu, wd = weights
    n, d = a.shape
    ff = act.shape[1]
    parts, steps, states = n // tokens, ff // tile, h is not None
    column = lambda i: jnp.maximum(i - 4, 0) // parts
    part = lambda i: jnp.maximum(i - 4, 0) % parts
    saved = pl.BlockSpec((tokens, tile), lambda i: (part(i), column(i)))
    rows_of = pl.BlockSpec((None, tile, d), lambda i: (number, column(i), 0))
    columns_of = pl.BlockSpec((None, d, tile), lambda i: (number, 0, column(i)))
    dma = pltpu.SemaphoreType.DMA
    v = lambda *shape: pltpu.VMEM(shape, BF)
    f = lambda *shape: pltpu.VMEM(shape, F32)
    r, q = ff // 8, ff // 16
    down_scratch = [v(2, 2, r, d)] * 3 + [f(2, q, d)] * 2 + [v(2, q, d)] * 4 + [v(q, d)] * 4
    p = d // 8
    pair_scratch = [v(2, 2, p, tile)] * 2 + [v(2, 2, 2, p, tile), f(2, 2, p, tile)]
    pair_scratch += [v(2, p, tile), v(steps, 2, p, tile), v(2, p, tile), v(steps, p, tile)]
    sems = [dma((2, 4)), dma((2, 4)), dma((2, 2, 2)), dma((2, 4, steps))]
    return pl.pallas_call(
        functools.partial(backward_kernel, states, tokens, tile, steps),
        grid=(4 + steps * parts,),
        in_specs=[
            whole((n, d)),
            whole((n, d)),
            pl.BlockSpec((n, ff // 4), lambda i: (0, jnp.minimum(i, 3))),
            saved,
            saved,
            rows_of,
        ]
        + ([pl.BlockSpec(memory_space=pl.ANY), columns_of, columns_of] if states else [whole((8, 128))]),
        out_specs=[whole((p, ff)), whole((p, ff)), whole((r, d)), whole((8, 128))] + [pl.BlockSpec(memory_space=pl.ANY)] * states,
        out_shape=[sds((p, ff), BF), sds((p, ff), BF), sds((r, d), BF), sds((8, 128), F32)]
        + [sds((n, d), BF)] * states,
        scratch_shapes=[v(n, tile)] * 2 + down_scratch + pair_scratch * 2 + sems
        + ([f(n, d), v(2, 256, d), v(2, 256, d), dma((2,)), dma((2,))] if states else [f(8, 128), f(8, 8, 128), dma((2, 8))]),
        compiler_params=pltpu.CompilerParams(
            vmem_limit_bytes=VMEM, collective_id=number, has_side_effects=True
        ),
        cost_estimate=cost(6 if states else 4, n, d, ff, 12 * n * ff),
        name="backward",
    )(a, dy, act, sa, sb, wd, *([h, wg, wu] if states else [before]))


def swap(value, bit):
    return lax.ppermute(value, "dp", [(i, i ^ bit) for i in range(8)])


def adamw_kernel(count, me_ref, squares_ref, g0_ref, g1_ref, w_ref, m_ref, v_ref, wo_ref, mo_ref, vo_ref):
    factor = jnp.minimum(1.0, 0.5 * lax.rsqrt(squares_ref[0:1, 0:1] / count + 1e-30))
    g = jnp.where(pl.program_id(0) == 0, g0_ref[...].astype(F32), g1_ref[...].astype(F32)) * factor
    m = 0.9 * m_ref[...] + 0.1 * g
    v = 0.95 * v_ref[...] + 0.05 * g * g
    step = m * lax.rsqrt(v + 1e-8) + 0.1 * w_ref[...].astype(F32)
    wo_ref[...] = (w_ref[...].astype(F32) - 0.02 * step).astype(BF)
    mo_ref[...], vo_ref[...] = m, v


def adamw(me, squares, count, g0, g1, w, m, v):
    _, rows, columns = m.shape
    by_columns = rows < 128
    block = (rows, columns // PARTS) if by_columns else (rows // PARTS, columns)
    at = (lambda c: (0, c)) if by_columns else (lambda c: (c, 0))
    grad = pl.BlockSpec(block, lambda l, c, s: at(c))
    state = pl.BlockSpec((None, *block), lambda l, c, s: (l, *at(c)))
    mine = (lambda l, c, s: (l, s[0], c)) if by_columns else (lambda l, c, s: (l, s[0] * PARTS + c, 0))
    return pl.pallas_call(
        functools.partial(adamw_kernel, count),
        grid_spec=pltpu.PrefetchScalarGridSpec(
            num_scalar_prefetch=1,
            grid=(2, PARTS),
            in_specs=[whole((8, 128)), grad, grad, pl.BlockSpec((None, *block), mine), state, state],
            out_specs=[state] * 3,
        ),
        out_shape=[sds(m.shape, BF), sds(m.shape, F32), sds(m.shape, F32)],
        compiler_params=params(),
        cost_estimate=pl.CostEstimate(flops=m.size * 4000, bytes_accessed=m.size * 22, transcendentals=0),
        name="adamw",
    )(me, squares, g0, g1, w, m, v)


def place_kernel(pieces, *refs):
    refs = list(refs)
    blocks, out = refs[: len(pieces)], refs[-3]
    buffer, sems = refs[-2], refs[-1]
    (x, y, core), _ = peers()
    todo = []
    at = 0
    for (bit, off), block in zip(pieces, blocks, strict=True):
        rows = block.shape[1]
        slot = 4 * xor(x, bit // 4) + 2 * xor(y, bit // 2 % 2) + xor(core, bit % 2)
        for number in range(block.shape[0]):
            k = len(todo)
            held = buffer.at[pl.ds(at, rows)]
            at += rows
            todo.append(
                (
                    pltpu.make_async_copy(block.at[number], held, sems.at[0, k]),
                    pltpu.make_async_copy(held, out.at[number, slot, pl.ds(off, rows)], sems.at[1, k]),
                )
            )
    for fetch, _ in todo:
        fetch.start()
    for fetch, store in todo:
        fetch.wait()
        store.start()
    for _, store in todo:
        store.wait()


def place(pieces, blocks, into=None, shape=None):
    layers, columns = blocks[0].shape[0], blocks[0].shape[2]
    anywhere = pl.BlockSpec(memory_space=pl.ANY)
    total_rows = layers * sum(b.shape[1] for b in blocks)
    size = 4 * total_rows * columns
    return pl.pallas_call(
        functools.partial(place_kernel, pieces),
        in_specs=[anywhere] * (len(blocks) + (into is not None)),
        out_specs=anywhere,
        out_shape=sds(shape, BF),
        scratch_shapes=[pltpu.VMEM((total_rows, columns), BF), pltpu.SemaphoreType.DMA((2, layers * len(blocks)))],
        input_output_aliases={len(blocks): 0} if into is not None else {},
        compiler_params=params(),
        cost_estimate=pl.CostEstimate(flops=size * 300, bytes_accessed=size, transcendentals=0),
        name="place",
    )(*blocks, *([into] if into is not None else []))


def all_gather(mine):
    done = []
    for w in mine:
        half = w.shape[1] // 32 * 16
        bx, by, bc = (swap(w, bit) for bit in (X, Y, CORE))
        fa = swap(bx[:, :half], Y)
        fb = swap(by[:, half:], X)
        cx, cy = (swap(t, CORE) for t in (bx, by))
        shape = (w.shape[0], 8, *w.shape[1:])
        near = ((0, 0), (1, 0), (4, 0), (5, 0), (2, 0), (3, 0))
        out = place(near, (w, bc, bx, cx, by, cy), None, shape)
        ca, cb = (swap(t, CORE) for t in (fa, fb))
        rest = ((6, 0), (7, 0), (6, half), (7, half))
        out = place(rest, (fa, ca, fb, cb), out, shape)
        done.append(out.reshape(w.shape[0], -1, w.shape[2]))
    return done


def solution(mesh):
    def step(x, dy, *arrays):
        weights, ms, vs = (arrays[i : i + 3] for i in (0, 3, 6))
        h0, dy = x[0], dy[0]
        me = lax.axis_index("dp").astype(jnp.int32).reshape(1)
        a0, act0, sa0, sb0, h1 = forward(0, h0, weights, True)
        a1, act1, sa1, sb1 = forward(1, h1, weights, False)
        *second, squares, dh1 = backward(1, a1, dy, act1, sa1, sb1, weights, h1)
        *first, squares = backward(0, a0, dh1, act0, sa0, sb0, weights, before=squares, tokens=1024)
        count = sum(w.size for w in weights)
        new = [adamw(me, squares, count, *args) for args in zip(first, second, weights, ms, vs, strict=True)]
        whole_weights = all_gather([w for w, _, _ in new])
        return (*whole_weights, *(m for _, m, _ in new), *(v for _, _, v in new))

    batch, rows = P(("rep", "dp")), P(None, "dp")
    return jax.shard_map(
        step,
        mesh=mesh,
        in_specs=(batch,) * 2 + (P(),) * 3 + (rows,) * 6,
        out_specs=(P("rep"),) * 3 + (P("rep", "dp"),) * 6,
        check_vma=False,
    )
```

profile of v0, /device:TPU:0, one launch (start us, length us, event | category | flops | bytes accessed | tf_op | source)
XLA Modules:
  0.0 437.3 jit_solution(9042515419518205088)
XLA Ops:
  0.6 43.4 %forward.2 = (bf16[2048,896]{1,0:T(8,128)(2,1)}, bf16[2048,2560]{1,0:T(8,128)(2,1)}, f32[2048,2560]{1,0:T(8,128)}, f32[2048,2560]{1,0:T(8,128)}, bf16[2048,896]{1,0:T(8,128)(2,1)}) custom-call(bf16[2048,896]{1,0:T(8,128)(2,1)} %bitcast.9, bf16[2,896,2560]{2,1,0:T(8,128)(2,1)} %w_ref.3, bf16[2,896,2560]{2,1,0:T(8,128)(2,1)} %w_ref.4, bf16[2,2560,896]{2,1,0:T(8,128)(2,1)} %w_ref.5), custom_call_target="tpu_custom_call" | custom-call | flops 28185722880 | bytes 52428800 | tf_op jit(solution)/shard_map/forward/pallas_call | solution.py:68
  44.1 31.4 %forward.3 = (bf16[2048,896]{1,0:T(8,128)(2,1)}, bf16[2048,2560]{1,0:T(8,128)(2,1)}, f32[2048,2560]{1,0:T(8,128)}, f32[2048,2560]{1,0:T(8,128)}) custom-call(bf16[2048,896]{1,0:T(8,128)(2,1)} %get-tuple-element.37.h_ref.refs_6_, bf16[2,896,2560]{2,1,0:T(8,128)(2,1)} %w_ref.3, bf16[2,896,2560]{2,1,0:T(8,128)(2,1)} %w_ref.4), custom_call_target="tpu_custom_call" | custom-call | flops 18790481920 | bytes 52428800 | tf_op jit(solution)/shard_map/forward/pallas_call | solution.py:68
  75.4 106.3 %backward.2 = (bf16[112,2560]{1,0:T(8,128)(2,1)}, bf16[112,2560]{1,0:T(8,128)(2,1)}, bf16[320,896]{1,0:T(8,128)(2,1)}, f32[8,128]{1,0:T(8,128)}, bf16[2048,896]{1,0:T(8,128)(2,1)}) custom-call(bf16[2048,896]{1,0:T(8,128)(2,1)} %get-tuple-element.38.refs_0_, bf16[2048,896]{1,0:T(8,128)(2,1)} %bitcast.10, bf16[2048,2560]{1,0:T(8,128)(2,1)} %get-tuple-element.39.refs_2_, ...), custom_call_target="tpu_custom_call" | custom-call | flops 56371445760 | bytes 62914560 | tf_op jit(solution)/shard_map/backward/pallas_call | solution.py:336
  181.8 91.2 %backward.3 = (bf16[112,2560]{1,0:T(8,128)(2,1)}, bf16[112,2560]{1,0:T(8,128)(2,1)}, bf16[320,896]{1,0:T(8,128)(2,1)}, f32[8,128]{1,0:T(8,128)}) custom-call(bf16[2048,896]{1,0:T(8,128)(2,1)} %get-tuple-element.36.refs_0_, bf16[2048,896]{1,0:T(8,128)(2,1)} %get-tuple-element.42.refs_1_, bf16[2048,2560]{1,0:T(8,128)(2,1)} %get-tuple-element.43.refs_2_, ...), custom_call_target="tpu_custom_call" | custom-call | flops 37580963840 | bytes 62914560 | tf_op jit(solution)/shard_map/backward/pallas_call | solution.py:336
  272.9 6.7 %adamw.5 = (bf16[2,320,896]{2,1,0:T(8,128)(2,1)}, f32[2,320,896]{2,1,0:T(8,128)}, f32[2,320,896]{2,1,0:T(8,128)}) custom-call(s32[1]{0:T(128)} %bitcast.me_ref, f32[8,128]{1,0:T(8,128)} %get-tuple-element.47.squares_ref, bf16[320,896]{1,0:T(8,128)(2,1)} %get-tuple-element.54.g0_ref, bf16[320,896]{1,0:T(8,128)(2,1)} %get-tuple-element.55.g1_ref, ...), custom_call_target="tpu_custom_call" | custom-call | flops 2293760000 | bytes 12615680 | tf_op jit(solution)/shard_map/adamw/pallas_call | solution.py:383
  279.6 1.5 collective-permute-start.18
  281.6 6.7 %adamw.4 = (bf16[2,112,2560]{2,1,0:T(8,128)(2,1)}, f32[2,112,2560]{2,1,0:T(8,128)}, f32[2,112,2560]{2,1,0:T(8,128)}) custom-call(s32[1]{0:T(128)} %bitcast.me_ref, f32[8,128]{1,0:T(8,128)} %get-tuple-element.47.squares_ref, bf16[112,2560]{1,0:T(8,128)(2,1)} %get-tuple-element.51.g0_ref, bf16[112,2560]{1,0:T(8,128)(2,1)} %get-tuple-element.52.g1_ref, ...), custom_call_target="tpu_custom_call" | custom-call | flops 2293760000 | bytes 12615680 | tf_op jit(solution)/shard_map/adamw/pallas_call | solution.py:383
  288.3 1.6 collective-permute-start.9
  289.9 6.7 %adamw.3 = (bf16[2,112,2560]{2,1,0:T(8,128)(2,1)}, f32[2,112,2560]{2,1,0:T(8,128)}, f32[2,112,2560]{2,1,0:T(8,128)}) custom-call(s32[1]{0:T(128)} %bitcast.me_ref, f32[8,128]{1,0:T(8,128)} %get-tuple-element.47.squares_ref, bf16[112,2560]{1,0:T(8,128)(2,1)} %get-tuple-element.48.g0_ref, bf16[112,2560]{1,0:T(8,128)(2,1)} %get-tuple-element.49.g1_ref, ...), custom_call_target="tpu_custom_call" | custom-call | flops 2293760000 | bytes 12615680 | tf_op jit(solution)/shard_map/adamw/pallas_call | solution.py:383
  297.0 11.0 %collective-permute-done.18.refs_2_ = bf16[2,320,896]{2,1,0:T(8,128)(2,1)} collective-permute-done((bf16[2,320,896]{2,1,0:T(8,128)(2,1)}, bf16[2,320,896]{2,1,0:T(8,128)(2,1)}, u32[]{:S(2)}, u32[]{:S(2)}) %collective-permute-start.18) | collective-permute-done | bytes 1146912 | tf_op jit(solution)/shard_map/ppermute | solution.py:362
  308.1 1.5 collective-permute-start.12
  310.1 22.5 %collective-permute-done.9.refs_2_ = bf16[2,112,2560]{2,1,0:T(8,128)(2,1)} collective-permute-done((bf16[2,112,2560]{2,1,0:T(8,128)(2,1)}, bf16[2,112,2560]{2,1,0:T(8,128)(2,1)}, u32[]{:S(2)}, u32[]{:S(2)}) %collective-permute-start.9) | collective-permute-done | bytes 1146912 | tf_op jit(solution)/shard_map/ppermute | solution.py:362
  333.7 22.7 %collective-permute-done.refs_2_ = bf16[2,112,2560]{2,1,0:T(8,128)(2,1)} collective-permute-done((bf16[2,112,2560]{2,1,0:T(8,128)(2,1)}, bf16[2,112,2560]{2,1,0:T(8,128)(2,1)}, u32[]{:S(2)}, u32[]{:S(2)}) %collective-permute-start) | collective-permute-done | bytes 1146912 | tf_op jit(solution)/shard_map/ppermute | solution.py:362
  356.4 1.5 collective-permute-start.10
  360.6 1.6 collective-permute-start.19
  362.2 1.1 slice.27
  363.8 6.6 %collective-permute-done.10.refs_0_ = bf16[2,48,2560]{2,1,0:T(8,128)(2,1)S(1)} collective-permute-done((bf16[2,48,2560]{2,1,0:T(8,128)(2,1)S(1)}, bf16[2,48,2560]{2,1,0:T(8,128)(2,1)S(1)}, u32[]{:S(2)}, u32[]{:S(2)}) %collective-permute-start.10) | collective-permute-done | bytes 491552 | tf_op jit(solution)/shard_map/ppermute | solution.py:362
  371.2 1.1 slice.29
  372.4 8.6 %collective-permute-done.1.refs_0_ = bf16[2,48,2560]{2,1,0:T(8,128)(2,1)S(1)} collective-permute-done((bf16[2,48,2560]{2,1,0:T(8,128)(2,1)S(1)}, bf16[2,48,2560]{2,1,0:T(8,128)(2,1)S(1)}, u32[]{:S(2)}, u32[]{:S(2)}) %collective-permute-start.1) | collective-permute-done | bytes 491552 | tf_op jit(solution)/shard_map/ppermute | solution.py:362
  381.8 1.5 collective-permute-start.22
  383.3 1.1 slice.25
  384.5 7.3 %collective-permute-done.19.refs_0_ = bf16[2,160,896]{2,1,0:T(8,128)(2,1)S(1)} collective-permute-done((bf16[2,160,896]{2,1,0:T(8,128)(2,1)S(1)}, bf16[2,160,896]{2,1,0:T(8,128)(2,1)S(1)}, u32[]{:S(2)}, u32[]{:S(2)}) %collective-permute-start.19) | collective-permute-done | bytes 573472 | tf_op jit(solution)/shard_map/ppermute | solution.py:362
  391.8 1.5 collective-permute-start.4
  393.3 1.5 collective-permute-done.22.refs_2_
  395.3 12.7 %collective-permute-done.4.refs_2_ = bf16[2,64,2560]{2,1,0:T(8,128)(2,1)} collective-permute-done((bf16[2,64,2560]{2,1,0:T(8,128)(2,1)S(1)}, bf16[2,64,2560]{2,1,0:T(8,128)(2,1)}, u32[]{:S(2)}, u32[]{:S(2)}) %collective-permute-start.4) | collective-permute-done | bytes 655392 | tf_op jit(solution)/shard_map/ppermute | solution.py:362
  408.6 1.4 collective-permute-done.20.refs_1_
  411.0 5.8 %place.10.refs_4_ = bf16[2,8,320,896]{3,2,1,0:T(8,128)(2,1)} custom-call(bf16[2,320,896]{2,1,0:T(8,128)(2,1)} %get-tuple-element.56.refs_0_, bf16[2,320,896]{2,1,0:T(8,128)(2,1)} %collective-permute-done.24.refs_1_, bf16[2,320,896]{2,1,0:T(8,128)(2,1)} %collective-permute-done.18.refs_2_, bf16[2,320,896]{2,1,0:T(8,128)(2,1)} %collective-permute-done.25.refs_3_, ...), custom_call_target="tpu_custom_call" | custom-call | flops 4128768000 | bytes 13762560 | tf_op jit(solution)/shard_map/place/pallas_call | solution.py:432
  417.3 5.8 %place.8.refs_4_ = bf16[2,8,112,2560]{3,2,1,0:T(8,128)(2,1)} custom-call(bf16[2,112,2560]{2,1,0:T(8,128)(2,1)} %get-tuple-element.53.refs_0_, bf16[2,112,2560]{2,1,0:T(8,128)(2,1)} %collective-permute-done.15.refs_1_, bf16[2,112,2560]{2,1,0:T(8,128)(2,1)} %collective-permute-done.9.refs_2_, bf16[2,112,2560]{2,1,0:T(8,128)(2,1)} %collective-permute-done.16.refs_3_, ...), custom_call_target="tpu_custom_call" | custom-call | flops 4128768000 | bytes 13762560 | tf_op jit(solution)/shard_map/place/pallas_call | solution.py:432
  423.5 2.5 place.11
  426.1 5.8 %place.6.refs_4_ = bf16[2,8,112,2560]{3,2,1,0:T(8,128)(2,1)} custom-call(bf16[2,112,2560]{2,1,0:T(8,128)(2,1)} %get-tuple-element.50.refs_0_, bf16[2,112,2560]{2,1,0:T(8,128)(2,1)} %collective-permute-done.6.refs_1_, bf16[2,112,2560]{2,1,0:T(8,128)(2,1)} %collective-permute-done.refs_2_, bf16[2,112,2560]{2,1,0:T(8,128)(2,1)} %collective-permute-done.7.refs_3_, ...), custom_call_target="tpu_custom_call" | custom-call | flops 4128768000 | bytes 13762560 | tf_op jit(solution)/shard_map/place/pallas_call | solution.py:432
  431.9 2.6 place.9
  434.5 2.6 place.7
  (49 shorter events, 10.5 us)
Async XLA Ops:
  279.6 28.5 %collective-permute-start.18 = (bf16[2,320,896]{2,1,0:T(8,128)(2,1)}, bf16[2,320,896]{2,1,0:T(8,128)(2,1)}, u32[]{:S(2)}, u32[]{:S(2)}) collective-permute-start(bf16[2,320,896]{2,1,0:T(8,128)(2,1)} %get-tuple-element.56.refs_0_), channel_id=1, source_target_pairs={{0,4},{1,5},{2,6},{3,7},{4,0},{5,1},{6,2},{7,3}} | collective-permute-start | bytes 3440648 | tf_op jit(solution)/shard_map/ppermute | solution.py:362
  281.1 28.5 %collective-permute-start.21 = (bf16[2,320,896]{2,1,0:T(8,128)(2,1)}, bf16[2,320,896]{2,1,0:T(8,128)(2,1)}, u32[]{:S(2)}, u32[]{:S(2)}) collective-permute-start(bf16[2,320,896]{2,1,0:T(8,128)(2,1)} %get-tuple-element.56.refs_0_), channel_id=1, source_target_pairs={{0,2},{1,3},{2,0},{3,1},{4,6},{5,7},{6,4},{7,5}} | collective-permute-start | bytes 3440648 | tf_op jit(solution)/shard_map/ppermute | solution.py:362
  281.6 28.0 %collective-permute-start.24 = (bf16[2,320,896]{2,1,0:T(8,128)(2,1)}, bf16[2,320,896]{2,1,0:T(8,128)(2,1)}, u32[]{:S(2)}, u32[]{:S(2)}) collective-permute-start(bf16[2,320,896]{2,1,0:T(8,128)(2,1)} %get-tuple-element.56.refs_0_), channel_id=1, source_target_pairs={{0,1},{1,0},{2,3},{3,2},{4,5},{5,4},{6,7},{7,6}} | collective-permute-start | bytes 3440648 | tf_op jit(solution)/shard_map/ppermute | solution.py:362
  288.3 44.3 %collective-permute-start.9 = (bf16[2,112,2560]{2,1,0:T(8,128)(2,1)}, bf16[2,112,2560]{2,1,0:T(8,128)(2,1)}, u32[]{:S(2)}, u32[]{:S(2)}) collective-permute-start(bf16[2,112,2560]{2,1,0:T(8,128)(2,1)} %get-tuple-element.53.refs_0_), channel_id=1, source_target_pairs={{0,4},{1,5},{2,6},{3,7},{4,0},{5,1},{6,2},{7,3}} | collective-permute-start | bytes 3440648 | tf_op jit(solution)/shard_map/ppermute | solution.py:362
  296.5 59.8 %collective-permute-start = (bf16[2,112,2560]{2,1,0:T(8,128)(2,1)}, bf16[2,112,2560]{2,1,0:T(8,128)(2,1)}, u32[]{:S(2)}, u32[]{:S(2)}) collective-permute-start(bf16[2,112,2560]{2,1,0:T(8,128)(2,1)} %get-tuple-element.50.refs_0_), channel_id=1, source_target_pairs={{0,4},{1,5},{2,6},{3,7},{4,0},{5,1},{6,2},{7,3}} | collective-permute-start | bytes 3440648 | tf_op jit(solution)/shard_map/ppermute | solution.py:362
  308.1 50.9 %collective-permute-start.12 = (bf16[2,112,2560]{2,1,0:T(8,128)(2,1)}, bf16[2,112,2560]{2,1,0:T(8,128)(2,1)}, u32[]{:S(2)}, u32[]{:S(2)}) collective-permute-start(bf16[2,112,2560]{2,1,0:T(8,128)(2,1)} %get-tuple-element.53.refs_0_), channel_id=1, source_target_pairs={{0,2},{1,3},{2,0},{3,1},{4,6},{5,7},{6,4},{7,5}} | collective-permute-start | bytes 3440648 | tf_op jit(solution)/shard_map/ppermute | solution.py:362
  309.6 51.0 %collective-permute-start.15 = (bf16[2,112,2560]{2,1,0:T(8,128)(2,1)}, bf16[2,112,2560]{2,1,0:T(8,128)(2,1)}, u32[]{:S(2)}, u32[]{:S(2)}) collective-permute-start(bf16[2,112,2560]{2,1,0:T(8,128)(2,1)} %get-tuple-element.53.refs_0_), channel_id=1, source_target_pairs={{0,1},{1,0},{2,3},{3,2},{4,5},{5,4},{6,7},{7,6}} | collective-permute-start | bytes 3440648 | tf_op jit(solution)/shard_map/ppermute | solution.py:362
  309.6 53.7 %collective-permute-start.3 = (bf16[2,112,2560]{2,1,0:T(8,128)(2,1)}, bf16[2,112,2560]{2,1,0:T(8,128)(2,1)}, u32[]{:S(2)}, u32[]{:S(2)}) collective-permute-start(bf16[2,112,2560]{2,1,0:T(8,128)(2,1)} %get-tuple-element.50.refs_0_), channel_id=1, source_target_pairs={{0,2},{1,3},{2,0},{3,1},{4,6},{5,7},{6,4},{7,5}} | collective-permute-start | bytes 3440648 | tf_op jit(solution)/shard_map/ppermute | solution.py:362
  332.6 31.2 %collective-permute-start.6 = (bf16[2,112,2560]{2,1,0:T(8,128)(2,1)}, bf16[2,112,2560]{2,1,0:T(8,128)(2,1)}, u32[]{:S(2)}, u32[]{:S(2)}) collective-permute-start(bf16[2,112,2560]{2,1,0:T(8,128)(2,1)} %get-tuple-element.50.refs_0_), channel_id=1, source_target_pairs={{0,1},{1,0},{2,3},{3,2},{4,5},{5,4},{6,7},{7,6}} | collective-permute-start | bytes 3440648 | tf_op jit(solution)/shard_map/ppermute | solution.py:362
  356.4 14.1 %collective-permute-start.10 = (bf16[2,48,2560]{2,1,0:T(8,128)(2,1)S(1)}, bf16[2,48,2560]{2,1,0:T(8,128)(2,1)S(1)}, u32[]{:S(2)}, u32[]{:S(2)}) collective-permute-start(bf16[2,48,2560]{2,1,0:T(8,128)(2,1)S(1)} %slice.26), channel_id=1, source_target_pairs={{0,2},{1,3},{2,0},{3,1},{4,6},{5,7},{6,4},{7,5}} | collective-permute-start | bytes 1474568 | tf_op jit(solution)/shard_map/ppermute | solution.py:362
  359.0 22.0 %collective-permute-start.1 = (bf16[2,48,2560]{2,1,0:T(8,128)(2,1)S(1)}, bf16[2,48,2560]{2,1,0:T(8,128)(2,1)S(1)}, u32[]{:S(2)}, u32[]{:S(2)}) collective-permute-start(bf16[2,48,2560]{2,1,0:T(8,128)(2,1)S(1)} %slice.24), channel_id=1, source_target_pairs={{0,2},{1,3},{2,0},{3,1},{4,6},{5,7},{6,4},{7,5}} | collective-permute-start | bytes 1474568 | tf_op jit(solution)/shard_map/ppermute | solution.py:362
  360.6 31.2 %collective-permute-start.19 = (bf16[2,160,896]{2,1,0:T(8,128)(2,1)S(1)}, bf16[2,160,896]{2,1,0:T(8,128)(2,1)S(1)}, u32[]{:S(2)}, u32[]{:S(2)}) collective-permute-start(bf16[2,160,896]{2,1,0:T(8,128)(2,1)S(1)} %slice.28), channel_id=1, source_target_pairs={{0,2},{1,3},{2,0},{3,1},{4,6},{5,7},{6,4},{7,5}} | collective-permute-start | bytes 1720328 | tf_op jit(solution)/shard_map/ppermute | solution.py:362
  363.3 31.5 %collective-permute-start.13 = (bf16[2,64,2560]{2,1,0:T(8,128)(2,1)S(1)}, bf16[2,64,2560]{2,1,0:T(8,128)(2,1)}, u32[]{:S(2)}, u32[]{:S(2)}) collective-permute-start(bf16[2,64,2560]{2,1,0:T(8,128)(2,1)S(1)} %slice.27), channel_id=1, source_target_pairs={{0,4},{1,5},{2,6},{3,7},{4,0},{5,1},{6,2},{7,3}} | collective-permute-start | bytes 1966088 | tf_op jit(solution)/shard_map/ppermute | solution.py:362
  363.8 44.2 %collective-permute-start.25 = (bf16[2,320,896]{2,1,0:T(8,128)(2,1)}, bf16[2,320,896]{2,1,0:T(8,128)(2,1)}, u32[]{:S(2)}, u32[]{:S(2)}) collective-permute-start(bf16[2,320,896]{2,1,0:T(8,128)(2,1)} %collective-permute-done.18.refs_2_), channel_id=1, source_target_pairs={{0,1},{1,0},{2,3},{3,2},{4,5},{5,4},{6,7},{7,6}} | collective-permute-start | bytes 3440648 | tf_op jit(solution)/shard_map/ppermute | solution.py:362
  370.5 0.8 copy-start.3
  371.2 37.3 %collective-permute-start.26 = (bf16[2,320,896]{2,1,0:T(8,128)(2,1)}, bf16[2,320,896]{2,1,0:T(8,128)(2,1)}, u32[]{:S(2)}, u32[]{:S(2)}) collective-permute-start(bf16[2,320,896]{2,1,0:T(8,128)(2,1)} %collective-permute-done.21.refs_4_), channel_id=1, source_target_pairs={{0,1},{1,0},{2,3},{3,2},{4,5},{5,4},{6,7},{7,6}} | collective-permute-start | bytes 3440648 | tf_op jit(solution)/shard_map/ppermute | solution.py:362
  381.0 0.8 copy-start.2
  381.8 13.0 %collective-permute-start.22 = (bf16[2,160,896]{2,1,0:T(8,128)(2,1)S(1)}, bf16[2,160,896]{2,1,0:T(8,128)(2,1)}, u32[]{:S(2)}, u32[]{:S(2)}) collective-permute-start(bf16[2,160,896]{2,1,0:T(8,128)(2,1)S(1)} %slice.29), channel_id=1, source_target_pairs={{0,4},{1,5},{2,6},{3,7},{4,0},{5,1},{6,2},{7,3}} | collective-permute-start | bytes 1720328 | tf_op jit(solution)/shard_map/ppermute | solution.py:362
  391.8 16.3 %copy-start = (bf16[2,160,896]{2,1,0:T(8,128)(2,1)}, bf16[2,160,896]{2,1,0:T(8,128)(2,1)S(1)}, u32[]{:S(2)}) copy-start(bf16[2,160,896]{2,1,0:T(8,128)(2,1)S(1)} %collective-permute-done.19.refs_0_) | copy-start | bytes 1720324
  391.8 16.3 %collective-permute-start.4 = (bf16[2,64,2560]{2,1,0:T(8,128)(2,1)S(1)}, bf16[2,64,2560]{2,1,0:T(8,128)(2,1)}, u32[]{:S(2)}, u32[]{:S(2)}) collective-permute-start(bf16[2,64,2560]{2,1,0:T(8,128)(2,1)S(1)} %slice.25), channel_id=1, source_target_pairs={{0,4},{1,5},{2,6},{3,7},{4,0},{5,1},{6,2},{7,3}} | collective-permute-start | bytes 1966088 | tf_op jit(solution)/shard_map/ppermute | solution.py:362
  394.8 22.0 %collective-permute-start.16 = (bf16[2,112,2560]{2,1,0:T(8,128)(2,1)}, bf16[2,112,2560]{2,1,0:T(8,128)(2,1)}, u32[]{:S(2)}, u32[]{:S(2)}) collective-permute-start(bf16[2,112,2560]{2,1,0:T(8,128)(2,1)} %collective-permute-done.9.refs_2_), channel_id=1, source_target_pairs={{0,1},{1,0},{2,3},{3,2},{4,5},{5,4},{6,7},{7,6}} | collective-permute-start | bytes 3440648 | tf_op jit(solution)/shard_map/ppermute | solution.py:362
  394.8 22.4 %collective-permute-start.17 = (bf16[2,112,2560]{2,1,0:T(8,128)(2,1)}, bf16[2,112,2560]{2,1,0:T(8,128)(2,1)}, u32[]{:S(2)}, u32[]{:S(2)}) collective-permute-start(bf16[2,112,2560]{2,1,0:T(8,128)(2,1)} %collective-permute-done.12.refs_4_), channel_id=1, source_target_pairs={{0,1},{1,0},{2,3},{3,2},{4,5},{5,4},{6,7},{7,6}} | collective-permute-start | bytes 3440648 | tf_op jit(solution)/shard_map/ppermute | solution.py:362
  408.0 2.0 collective-permute-start.20
  408.1 17.9 %collective-permute-start.7 = (bf16[2,112,2560]{2,1,0:T(8,128)(2,1)}, bf16[2,112,2560]{2,1,0:T(8,128)(2,1)}, u32[]{:S(2)}, u32[]{:S(2)}) collective-permute-start(bf16[2,112,2560]{2,1,0:T(8,128)(2,1)} %collective-permute-done.refs_2_), channel_id=1, source_target_pairs={{0,1},{1,0},{2,3},{3,2},{4,5},{5,4},{6,7},{7,6}} | collective-permute-start | bytes 3440648 | tf_op jit(solution)/shard_map/ppermute | solution.py:362
  408.6 17.6 %collective-permute-start.8 = (bf16[2,112,2560]{2,1,0:T(8,128)(2,1)}, bf16[2,112,2560]{2,1,0:T(8,128)(2,1)}, u32[]{:S(2)}, u32[]{:S(2)}) collective-permute-start(bf16[2,112,2560]{2,1,0:T(8,128)(2,1)} %collective-permute-done.3.refs_4_), channel_id=1, source_target_pairs={{0,1},{1,0},{2,3},{3,2},{4,5},{5,4},{6,7},{7,6}} | collective-permute-start | bytes 3440648 | tf_op jit(solution)/shard_map/ppermute | solution.py:362
  410.0 0.8 copy-start.1
  410.9 12.2 %collective-permute-start.23 = (bf16[2,160,896]{2,1,0:T(8,128)(2,1)}, bf16[2,160,896]{2,1,0:T(8,128)(2,1)}, u32[]{:S(2)}, u32[]{:S(2)}) collective-permute-start(bf16[2,160,896]{2,1,0:T(8,128)(2,1)} %collective-permute-done.22.refs_2_), channel_id=1, source_target_pairs={{0,1},{1,0},{2,3},{3,2},{4,5},{5,4},{6,7},{7,6}} | collective-permute-start | bytes 1720328 | tf_op jit(solution)/shard_map/ppermute | solution.py:362
  416.8 15.1 %collective-permute-start.14 = (bf16[2,64,2560]{2,1,0:T(8,128)(2,1)}, bf16[2,64,2560]{2,1,0:T(8,128)(2,1)}, u32[]{:S(2)}, u32[]{:S(2)}) collective-permute-start(bf16[2,64,2560]{2,1,0:T(8,128)(2,1)} %collective-permute-done.13.refs_2_), channel_id=1, source_target_pairs={{0,1},{1,0},{2,3},{3,2},{4,5},{5,4},{6,7},{7,6}} | collective-permute-start | bytes 1966088 | tf_op jit(solution)/shard_map/ppermute | solution.py:362
  417.2 17.4 %collective-permute-start.5 = (bf16[2,64,2560]{2,1,0:T(8,128)(2,1)}, bf16[2,64,2560]{2,1,0:T(8,128)(2,1)}, u32[]{:S(2)}, u32[]{:S(2)}) collective-permute-start(bf16[2,64,2560]{2,1,0:T(8,128)(2,1)} %collective-permute-done.4.refs_2_), channel_id=1, source_target_pairs={{0,1},{1,0},{2,3},{3,2},{4,5},{5,4},{6,7},{7,6}} | collective-permute-start | bytes 1966088 | tf_op jit(solution)/shard_map/ppermute | solution.py:362
  423.1 8.8 %collective-permute-start.11 = (bf16[2,48,2560]{2,1,0:T(8,128)(2,1)}, bf16[2,48,2560]{2,1,0:T(8,128)(2,1)}, u32[]{:S(2)}, u32[]{:S(2)}) collective-permute-start(bf16[2,48,2560]{2,1,0:T(8,128)(2,1)} %copy-done.3), channel_id=1, source_target_pairs={{0,1},{1,0},{2,3},{3,2},{4,5},{5,4},{6,7},{7,6}} | collective-permute-start | bytes 1474568 | tf_op jit(solution)/shard_map/ppermute | solution.py:362
  426.0 8.6 %collective-permute-start.2 = (bf16[2,48,2560]{2,1,0:T(8,128)(2,1)}, bf16[2,48,2560]{2,1,0:T(8,128)(2,1)}, u32[]{:S(2)}, u32[]{:S(2)}) collective-permute-start(bf16[2,48,2560]{2,1,0:T(8,128)(2,1)} %copy-done.2), channel_id=1, source_target_pairs={{0,1},{1,0},{2,3},{3,2},{4,5},{5,4},{6,7},{7,6}} | collective-permute-start | bytes 1474568 | tf_op jit(solution)/shard_map/ppermute | solution.py:362
where the time goes:
time: 438 us; the launch traced here: 437 us
  Pallas kernels  317 us (72%)
  waiting for transfers between devices  94.5 us (22%)
  starting transfers between devices  15.6 us (4%)
  local copies, waits for them, and re-layouts  9.04 us (2%)
    pallas_call x2, Pallas kernels, backward(): pl.pallas_call(functools.partial(backward_kernel, states, tokens, tile, s...  197 us
    ppermute x27, waiting for transfers between devices, swap(): return lax.ppermute(value, 'dp', [(i, i ^ bit) for i in range(8)])  94.5 us
    pallas_call x2, Pallas kernels, forward(): pl.pallas_call(functools.partial(forward_kernel, chunk, down), grid=(n //...  74.8 us
    pallas_call x6, Pallas kernels, place(): pl.pallas_call(functools.partial(place_kernel, pieces), in_specs=[anywher...  24.9 us
    pallas_call x3, Pallas kernels, adamw(): pl.pallas_call(functools.partial(adamw_kernel, count), grid_spec=pltpu.Pr...  20 us
    ppermute x27, starting transfers between devices, swap(): return lax.ppermute(value, 'dp', [(i, i ^ bit) for i in range(8)])  15.6 us
  transfers between devices with their start and end apart: 27, of which 9 were waited for; matrix products, arithmetic and copies ran while one was open for 2% of the time, Pallas kernels for 8%

commit v1 on v0

--- a/solution.py
+++ b/solution.py
@@ -106,16 +106,20 @@
     refs = list(refs)
     take = lambda k: [refs.pop(0) for _ in range(k)]
     a_ref, dy_ref, act_ref, sa_ref, sb_ref, wd_ref = take(6)
-    h_ref, wg_ref, wu_ref = take(3) if states else (None,) * 3
-    (before_ref,) = (None,) if states else take(1)
-    gate_ref, up_ref, down_ref = take(3)
-    (squares_ref,) = take(1)
-    (dh_ref,) = take(1) if states else (None,)
-    dg_s, du_s = take(2)
+    if states:
+        h_ref, wg_ref, wu_ref = take(3)
+    else:
+        before_ref, left_ref, gate1_ref, up1_ref = take(4)
+    gate_ref, up_ref, down_ref, squares_ref = take(4)
+    if states:
+        dh_ref, left_ref = take(2)
+    else:
+        gate1_out, up1_out = take(2)
+    dg_s, du_s, act_s, act_sem = take(4)
     dk, do, di, da_sum, db_sum, dsx, dsy, drx, dry, dsy2, dsx2, dry2, drx2 = take(13)
     gk, go, gi, g_sum, gs1, gr1, gs2, gr2 = take(8)
     uk, uo, ui, u_sum, us1, ur1, us2, ur2 = take(8)
-    d_core, d_link, p_core, p_link = take(4)
+    d_core, d_link, p_core, p_link, left_sem = take(5)
     if states:
         da_s, h_s, dh_s, h_sem, dh_sem = take(5)
     else:
@@ -127,15 +131,32 @@
     (x, y, core), (to_core, to_y, to_x) = peers()
     mine = core == 0
 
-    def down_copy(q):
-        sx, sy = xor(q // 2, x), xor(q % 2, y)
-        return send(do.at[sx, sy], di.at[sx, sy], (d_core.at[0, q], d_core.at[1, q]), to_core)
-
-    def down_links(stage):
+    def other(k):
+        return 4 * xor(x, k // 4) + 2 * xor(y, k // 2 % 2) + xor(core, k % 2)
+
+    def start(copies):
+        for c in copies:
+            c.start()
+
+    def wait(copies):
+        for c in copies:
+            c.wait()
+
+    def down_copy(k):
+        slot = 1 - k // 2, 1 - k % 2
+        return send(do.at[slot], di.at[slot], (d_core.at[0, k], d_core.at[1, k]), to_core)
+
+    def fetch_act(k):
+        width = act_s.shape[2]
+        q = 2 * xor(1 - k // 2, x) + xor(1 - k % 2, y)
+        columns = pl.ds(pl.multiple_of(q * width, 128), width)
+        return pltpu.make_async_copy(act_ref.at[:, columns], act_s.at[k % 2], act_sem.at[k % 2])
+
+    def down_links(stage, way):
         sem = lambda k: (d_link.at[0, k], d_link.at[1, k])
         if stage == 1:
-            return send(dsx, drx, sem(0), to_x), send(dsy, dry, sem(1), to_y)
-        return send(dsy2, dry2, sem(2), to_y), send(dsx2, drx2, sem(3), to_x)
+            return send(dsx, drx, sem(0), to_x) if way == "x" else send(dsy, dry, sem(1), to_y)
+        return send(dsx2, drx2, sem(3), to_x) if way == "x" else send(dsy2, dry2, sem(2), to_y)
 
     def core_copy(which, u):
         src, dst = ((go, gi), (uo, ui))[which]
@@ -144,75 +165,89 @@
 
     def pair_links(stage, u):
         sem = lambda k: (p_link.at[0, k, u], p_link.at[1, k, u])
+        slot = u % 2
         if stage == 1:
-            return send(gs1, gr1.at[u], sem(0), to_x), send(us1, ur1.at[u], sem(1), to_y)
-        return send(gs2.at[u % 2], gr2.at[u], sem(2), to_y), send(us2.at[u % 2], ur2.at[u], sem(3), to_x)
-
-    def start(copies):
-        for c in copies:
-            c.start()
-
-    def wait(copies):
-        for c in copies:
-            c.wait()
-
-    def other(k):
-        return 4 * xor(x, k // 4) + 2 * xor(y, k // 2 % 2) + xor(core, k % 2)
-
-    def square_sum():
-        return sum(jnp.sum(jnp.square(ref[...].astype(F32))) for ref in (gate_ref, up_ref, down_ref))
+            return send(gs1.at[slot], gr1.at[u], sem(0), to_x), send(us1.at[slot], ur1.at[u], sem(1), to_y)
+        return send(gs2.at[slot], gr2.at[u], sem(2), to_y), send(us2.at[slot], ur2.at[u], sem(3), to_x)
 
     half = dk.shape[2] // 2
     lo, hi = pl.ds(0, half), pl.ds(half, half)
 
-    def down_first():
-        wait([down_copy(q) for q in range(4)])
+    def down_x():
+        wait([down_copy(0), down_copy(1)])
         dsx[...] = total(dk[1, :, lo], di[1, :, lo]).astype(BF)
+        down_links(1, "x").start()
+
+    def down_y():
+        wait([down_copy(2)])
         dsy[...] = total(dk[:, 1, hi], di[:, 1, hi]).astype(BF)
-        start(down_links(1))
+        down_links(1, "y").start()
+
+    def down_sums():
+        wait([down_copy(3)])
         da_sum[...] = total(dk[0, :, lo], di[0, :, lo])
         db_sum[...] = total(dk[:, 0, hi], di[:, 0, hi])
 
     def down_second():
-        wait(down_links(1))
+        down_links(1, "x").wait()
         dsy2[...] = total(da_sum[1], drx[1]).astype(BF)
+        down_links(2, "y").start()
+        da_sum[0] = total(da_sum[0], drx[0])
+        down_links(1, "y").wait()
         dsx2[...] = total(db_sum[1], dry[1]).astype(BF)
-        start(down_links(2))
-        da_sum[0] = total(da_sum[0], drx[0])
+        down_links(2, "x").start()
         db_sum[0] = total(db_sum[0], dry[0])
 
     def down_last():
-        wait(down_links(2))
+        down_links(2, "y").wait()
+        down_links(2, "x").wait()
         down_ref[lo, :] = total(da_sum[0], dry2[...]).astype(BF)
         down_ref[hi, :] = total(db_sum[0], drx2[...]).astype(BF)
 
     def pair_first(u):
-        slot = u % 2
+        slot, held = u % 2, u % 3
         wait([core_copy(0, u), core_copy(1, u)])
-        gs1[...] = total(gk[1], gi[slot, 1]).astype(BF)
-        us1[...] = total(uk[:, 1], ui[slot, :, 1]).astype(BF)
+        gs1[slot] = total(gk[1], gi[slot, 1]).astype(BF)
+        us1[slot] = total(uk[:, 1], ui[slot, :, 1]).astype(BF)
         start(pair_links(1, u))
-        g_sum[slot] = total(gk[0], gi[slot, 0])
-        u_sum[slot] = total(uk[:, 0], ui[slot, :, 0])
+        g_sum[held] = total(gk[0], gi[slot, 0])
+        u_sum[held] = total(uk[:, 0], ui[slot, :, 0])
 
     def pair_second(u):
-        slot = u % 2
+        slot, held = u % 2, u % 3
         wait(pair_links(1, u))
-        gs2[slot] = total(g_sum[slot, 1], gr1[u, 1]).astype(BF)
-        us2[slot] = total(u_sum[slot, 1], ur1[u, 1]).astype(BF)
+        gs2[slot] = total(g_sum[held, 1], gr1[u, 1]).astype(BF)
+        us2[slot] = total(u_sum[held, 1], ur1[u, 1]).astype(BF)
         start(pair_links(2, u))
-        g_sum[slot, 0] = total(g_sum[slot, 0], gr1[u, 0])
-        u_sum[slot, 0] = total(u_sum[slot, 0], ur1[u, 0])
-
-    def pair_last(u):
-        slot = u % 2
+        g_sum[held, 0] = total(g_sum[held, 0], gr1[u, 0])
+        u_sum[held, 0] = total(u_sum[held, 0], ur1[u, 0])
+
+    def pair_last(u, gate_to=None, up_to=None, column=None):
+        held = u % 3
         wait(pair_links(2, u))
-        cols = pl.ds(pl.multiple_of(u * tile, tile), tile)
-        gate_ref[:, cols] = total(g_sum[slot, 0], gr2[u]).astype(BF)
-        up_ref[:, cols] = total(u_sum[slot, 0], ur2[u]).astype(BF)
+        column = u if column is None else column
+        cols = pl.ds(pl.multiple_of(column * tile, tile), tile)
+        gate_to, up_to = (gate_ref, up_ref) if gate_to is None else (gate_to, up_to)
+        gate_to[:, cols] = total(g_sum[held, 0], gr2[u]).astype(BF)
+        up_to[:, cols] = total(u_sum[held, 0], ur2[u]).astype(BF)
+
+    def left_copies(fill):
+        held = (gk, go, uk, uo)
+        ends = [(left_ref.at[k], t) if fill else (t, left_ref.at[k]) for k, t in enumerate(held)]
+        return [pltpu.make_async_copy(src, dst, left_sem.at[k]) for k, (src, dst) in enumerate(ends)]
+
+    def squares_of(*values):
+        return sum(jnp.sum(jnp.square(value.astype(F32))) for value in values)
+
+    given = steps
+    most = (steps - 1) * tile
 
     @pl.when(i == 0)
     def _():
+        fetch_act(0).start()
+        fetch_act(1).start()
+        if not states:
+            start(left_copies(True))
         barrier = pltpu.get_barrier_semaphore()
         met = (to_core, to_y, to_x) if states else [other(k) for k in range(1, 8)]
         for to in met:
@@ -225,15 +260,28 @@
                 return 0
 
             lax.fori_loop(0, n // 256, clear, 0)
+        else:
+            wait(left_copies(True))
+            core_copy(0, given).start()
+            core_copy(1, given).start()
+            gate1_out[:, :most] = gate1_ref[:, :most]
+            up1_out[:, :most] = up1_ref[:, :most]
 
     @pl.when(i < 4)
     def _():
-        g = dot(act_ref[...], dy_ref[...], 0, 0)
+        fetch_act(i).wait()
+        g = dot(act_s[i % 2], dy_ref[...], 0, 0)
         rows = g.shape[0] // 2
-        sx, sy = xor(i // 2, x), xor(i % 2, y)
+        sx, sy = 1 - i // 2, 1 - i % 2
         dk[sx, sy] = jnp.where(mine, g[:rows], g[rows:]).astype(BF)
         do[sx, sy] = jnp.where(mine, g[rows:], g[:rows]).astype(BF)
         down_copy(i).start()
+        pl.when(i < 2)(lambda: fetch_act(i + 2).start())
+        if not states:
+            pl.when(i == 1)(lambda: pair_first(given))
+            pl.when(i == 3)(lambda: pair_second(given))
+        pl.when(i == 2)(down_x)
+        pl.when(i == 3)(down_y)
 
     @pl.when(i >= 4)
     def _():
@@ -248,12 +296,14 @@
 
         @pl.when(t == parts - 1)
         def _():
-            pl.when(j == 0)(down_first)
-            pl.when(j == 2)(down_second)
+            pl.when(j == 0)(down_sums)
+            pl.when(j >= 1)(lambda: pair_first(j - 1))
+            pl.when(j == 1)(down_second)
             pl.when(j >= 2)(lambda: pair_second(j - 2))
+            if not states:
+                pl.when(j == 1)(lambda: pair_last(given, gate1_out, up1_out, steps - 1))
+            pl.when(j == 2)(down_last)
             pl.when(j >= 3)(lambda: pair_last(j - 3))
-            pl.when(j >= 1)(lambda: pair_first(j - 1))
-            pl.when(j == 3)(down_last)
             rows = d // 8
             for which, (by, keep, out) in enumerate(((dg_s, gk, go), (du_s, uk, uo))):
                 g = dot(a_ref[...], by[...], 0, 0)
@@ -262,14 +312,16 @@
                     sx, sy = xor(q // 2, x), xor(q % 2, y)
                     keep[sx, sy] = jnp.where(mine, first, second).astype(BF)
                     out[sx, sy] = jnp.where(mine, second, first).astype(BF)
-                core_copy(which, j).start()
+                if states:
+                    pl.when(j < steps - 1)(lambda: core_copy(which, j).start())
+                else:
+                    core_copy(which, j).start()
 
     @pl.when(i == 4 + steps * parts - 1)
     def _():
-        pair_second(steps - 2)
-        pair_last(steps - 3)
-        pair_first(steps - 1)
         if states:
+            start(left_copies(False))
+            pair_second(steps - 2)
 
             def fetch(t):
                 rows = pl.ds(pl.multiple_of(t * 256, 256), 256)
@@ -295,15 +347,22 @@
                 return 0
 
             lax.fori_loop(0, n // 256, back, 0)
+            pair_last(steps - 3)
+            pair_last(steps - 2)
             store(n // 256 - 2).wait()
             store(n // 256 - 1).wait()
+            wait(left_copies(False))
+            squares = squares_of(gate_ref[:, :most], up_ref[:, :most], down_ref[...])
+            squares_ref[...] = jnp.full(squares_ref.shape, squares, F32)
+            return
+        pair_first(steps - 1)
+        pair_second(steps - 2)
+        pair_last(steps - 3)
+        known = before_ref[...] + squares_of(gate1_out[:, most:], up1_out[:, most:], down_ref[...])
         pair_second(steps - 1)
         pair_last(steps - 2)
         pair_last(steps - 1)
-        if states:
-            squares_ref[...] = jnp.full(squares_ref.shape, square_sum(), F32)
-            return
-        sq_s[...] = before_ref[...] + square_sum()
+        sq_s[...] = known + squares_of(gate_ref[...], up_ref[...])
         copies = [send(sq_s, sq_in.at[k], (sq_sem.at[0, k], sq_sem.at[1, k]), other(k)) for k in range(1, 8)]
         start(copies)
         wait(copies)
@@ -314,7 +373,7 @@
         squares_ref[...] = parts_of[0]
 
 
-def backward(number, a, dy, act, sa, sb, weights, h=None, before=None, tokens=512, tile=512):
+def backward(number, a, dy, act, sa, sb, weights, h=None, after=None, tokens=512, tile=512):
     wg, wu, wd = weights
     n, d = a.shape
     ff = act.shape[1]
@@ -324,38 +383,43 @@
     saved = pl.BlockSpec((tokens, tile), lambda i: (part(i), column(i)))
     rows_of = pl.BlockSpec((None, tile, d), lambda i: (number, column(i), 0))
     columns_of = pl.BlockSpec((None, d, tile), lambda i: (number, 0, column(i)))
+    anywhere = pl.BlockSpec(memory_space=pl.ANY)
     dma = pltpu.SemaphoreType.DMA
     v = lambda *shape: pltpu.VMEM(shape, BF)
     f = lambda *shape: pltpu.VMEM(shape, F32)
-    r, q = ff // 8, ff // 16
+    r, q, p = ff // 8, ff // 16, d // 8
+    units = steps if states else steps + 1
     down_scratch = [v(2, 2, r, d)] * 3 + [f(2, q, d)] * 2 + [v(2, q, d)] * 4 + [v(q, d)] * 4
-    p = d // 8
-    pair_scratch = [v(2, 2, p, tile)] * 2 + [v(2, 2, 2, p, tile), f(2, 2, p, tile)]
-    pair_scratch += [v(2, p, tile), v(steps, 2, p, tile), v(2, p, tile), v(steps, p, tile)]
-    sems = [dma((2, 4)), dma((2, 4)), dma((2, 2, 2)), dma((2, 4, steps))]
+    pair_scratch = [v(2, 2, p, tile)] * 2 + [v(2, 2, 2, p, tile), f(3, 2, p, tile)]
+    pair_scratch += [v(2, 2, p, tile), v(units, 2, p, tile), v(2, p, tile), v(units, p, tile)]
+    sems = [dma((2, 4)), dma((2, 4)), dma((2, 2, 2)), dma((2, 4, units)), dma((4,))]
+    left = sds((4, 2, 2, p, tile), BF)
+    if states:
+        more, more_specs = [h, wg, wu], [anywhere, columns_of, columns_of]
+        also, also_specs = [sds((n, d), BF), left], [anywhere, anywhere]
+        scratch = [f(n, d), v(2, 256, d), v(2, 256, d), dma((2,)), dma((2,))]
+    else:
+        more, more_specs = list(after), [whole((8, 128)), anywhere, whole((p, ff)), whole((p, ff))]
+        also, also_specs = [sds((p, ff), BF)] * 2, [whole((p, ff))] * 2
+        scratch = [f(8, 128), f(8, 8, 128), dma((2, 8))]
     return pl.pallas_call(
         functools.partial(backward_kernel, states, tokens, tile, steps),
         grid=(4 + steps * parts,),
-        in_specs=[
-            whole((n, d)),
-            whole((n, d)),
-            pl.BlockSpec((n, ff // 4), lambda i: (0, jnp.minimum(i, 3))),
-            saved,
-            saved,
-            rows_of,
-        ]
-        + ([pl.BlockSpec(memory_space=pl.ANY), columns_of, columns_of] if states else [whole((8, 128))]),
-        out_specs=[whole((p, ff)), whole((p, ff)), whole((r, d)), whole((8, 128))] + [pl.BlockSpec(memory_space=pl.ANY)] * states,
-        out_shape=[sds((p, ff), BF), sds((p, ff), BF), sds((r, d), BF), sds((8, 128), F32)]
-        + [sds((n, d), BF)] * states,
-        scratch_shapes=[v(n, tile)] * 2 + down_scratch + pair_scratch * 2 + sems
-        + ([f(n, d), v(2, 256, d), v(2, 256, d), dma((2,)), dma((2,))] if states else [f(8, 128), f(8, 8, 128), dma((2, 8))]),
+        in_specs=[whole((n, d)), whole((n, d)), anywhere, saved, saved, rows_of] + more_specs,
+        out_specs=[whole((p, ff)), whole((p, ff)), whole((r, d)), whole((8, 128))] + also_specs,
+        out_shape=[sds((p, ff), BF), sds((p, ff), BF), sds((r, d), BF), sds((8, 128), F32)] + also,
+        scratch_shapes=[v(n, tile)] * 2
+        + [v(2, n, ff // 4), dma((2,))]
+        + down_scratch
+        + pair_scratch * 2
+        + sems
+        + scratch,
         compiler_params=pltpu.CompilerParams(
             vmem_limit_bytes=VMEM, collective_id=number, has_side_effects=True
         ),
         cost_estimate=cost(6 if states else 4, n, d, ff, 12 * n * ff),
         name="backward",
-    )(a, dy, act, sa, sb, wd, *([h, wg, wu] if states else [before]))
+    )(a, dy, act, sa, sb, wd, *more)
 
 
 def swap(value, bit):
@@ -467,8 +531,10 @@
         me = lax.axis_index("dp").astype(jnp.int32).reshape(1)
         a0, act0, sa0, sb0, h1 = forward(0, h0, weights, True)
         a1, act1, sa1, sb1 = forward(1, h1, weights, False)
-        *second, squares, dh1 = backward(1, a1, dy, act1, sa1, sb1, weights, h1)
-        *first, squares = backward(0, a0, dh1, act0, sa0, sb0, weights, before=squares, tokens=1024)
+        gate1, up1, down1, squares, dh1, left = backward(1, a1, dy, act1, sa1, sb1, weights, h1)
+        after = (squares, left, gate1, up1)
+        *first, squares, gate1, up1 = backward(0, a0, dh1, act0, sa0, sb0, weights, after=after, tokens=1024)
+        second = (gate1, up1, down1)
         count = sum(w.size for w in weights)
         new = [adamw(me, squares, count, *args) for args in zip(first, second, weights, ms, vs, strict=True)]
         whole_weights = all_gather([w for w, _, _ in new])

time: 438 us -> 427 us (0.975)
  Pallas kernels: 317 us -> 307 us
    pallas_call x2, Pallas kernels: 197 us -> 187 us  [backward(): pl.pallas_call(functools.partial(backward_kernel, states, tokens, tile, s...]
where the time goes in v1:
time: 427 us
  Pallas kernels  307 us (72%)
  waiting for transfers between devices  95.2 us (22%)
  starting transfers between devices  14.7 us (3%)
  local copies, waits for them, and re-layouts  9.04 us (2%)
    pallas_call x2, Pallas kernels, backward(): pl.pallas_call(functools.partial(backward_kernel, states, tokens, tile, s...  187 us
    ppermute x27, waiting for transfers between devices, swap(): return lax.ppermute(value, 'dp', [(i, i ^ bit) for i in range(8)])  95.2 us
    pallas_call x2, Pallas kernels, forward(): pl.pallas_call(functools.partial(forward_kernel, chunk, down), grid=(n //...  74.8 us
    pallas_call x6, Pallas kernels, place(): pl.pallas_call(functools.partial(place_kernel, pieces), in_specs=[anywher...  24.9 us
    pallas_call x3, Pallas kernels, adamw(): pl.pallas_call(functools.partial(adamw_kernel, count), grid_spec=pltpu.Pr...  20.1 us
    ppermute x27, starting transfers between devices, swap(): return lax.ppermute(value, 'dp', [(i, i ^ bit) for i in range(8)])  14.7 us
  transfers between devices with their start and end apart: 27, of which 9 were waited for; matrix products, arithmetic and copies ran while one was open for 2% of the time, Pallas kernels for 8%

profile of v1, /device:TPU:0, one launch (start us, length us, event | category | flops | bytes accessed | tf_op | source)
XLA Modules:
  0.0 426.5 jit_solution(14162169378128329320)
XLA Ops:
  0.6 43.4 %forward.2 = (bf16[2048,896]{1,0:T(8,128)(2,1)}, bf16[2048,2560]{1,0:T(8,128)(2,1)}, f32[2048,2560]{1,0:T(8,128)}, f32[2048,2560]{1,0:T(8,128)}, bf16[2048,896]{1,0:T(8,128)(2,1)}) custom-call(bf16[2048,896]{1,0:T(8,128)(2,1)} %bitcast.9, bf16[2,896,2560]{2,1,0:T(8,128)(2,1)} %w_ref.3, bf16[2,896,2560]{2,1,0:T(8,128)(2,1)} %w_ref.4, bf16[2,2560,896]{2,1,0:T(8,128)(2,1)} %w_ref.5), custom_call_target="tpu_custom_call" | custom-call | flops 28185722880 | bytes 52428800 | tf_op jit(solution)/shard_map/forward/pallas_call | solution.py:68
  44.1 31.4 %forward.3 = (bf16[2048,896]{1,0:T(8,128)(2,1)}, bf16[2048,2560]{1,0:T(8,128)(2,1)}, f32[2048,2560]{1,0:T(8,128)}, f32[2048,2560]{1,0:T(8,128)}) custom-call(bf16[2048,896]{1,0:T(8,128)(2,1)} %get-tuple-element.40.h_ref.refs_6_, bf16[2,896,2560]{2,1,0:T(8,128)(2,1)} %w_ref.3, bf16[2,896,2560]{2,1,0:T(8,128)(2,1)} %w_ref.4), custom_call_target="tpu_custom_call" | custom-call | flops 18790481920 | bytes 52428800 | tf_op jit(solution)/shard_map/forward/pallas_call | solution.py:68
  75.4 98.5 %backward.2 = (bf16[112,2560]{1,0:T(8,128)(2,1)}, bf16[112,2560]{1,0:T(8,128)(2,1)}, bf16[320,896]{1,0:T(8,128)(2,1)}, f32[8,128]{1,0:T(8,128)}, bf16[2048,896]{...) custom-call(bf16[2048,896]{1,0:T(8,128)(2,1)} %get-tuple-element.41.refs_0_, bf16[2048,896]{1,0:T(8,128)(2,1)} %bitcast.10, ...), custom_call_target="tpu_custom_call" | custom-call | flops 56371445760 | bytes 62914560 | tf_op jit(solution)/shard_map/backward/pallas_call | solution.py:405
  174.0 88.2 %backward.3 = (bf16[112,2560]{1,0:T(8,128)(2,1)}, bf16[112,2560]{1,0:T(8,128)(2,1)}, bf16[320,896]{1,0:T(8,128)(2,1)}, f32[8,128]{1,0:T(8,128)}, bf16[112,2560]{1,0:T(8,128)(2,1)}, /*index=5*/bf16[112,2560]{1,0:T(8,128)(2,1)}) custom-call(bf16[2048,896]{1,0:T(8,128)(2,1)} %get-tuple-element.39.refs_0_, bf16[2048,896]{1,0:T(8,128)(2,1)} %get-tuple-element.45.refs_1_, ...), custom_call_target="tpu_custom_call" | custom-call | flops 37580963840 | bytes 62914560 | tf_op jit(solution)/shard_map/backward/pallas_call | solution.py:405
  262.1 6.7 %adamw.5 = (bf16[2,320,896]{2,1,0:T(8,128)(2,1)}, f32[2,320,896]{2,1,0:T(8,128)}, f32[2,320,896]{2,1,0:T(8,128)}) custom-call(s32[1]{0:T(128)} %bitcast.me_ref, f32[8,128]{1,0:T(8,128)} %get-tuple-element.53.squares_ref, bf16[320,896]{1,0:T(8,128)(2,1)} %get-tuple-element.60.g0_ref, bf16[320,896]{1,0:T(8,128)(2,1)} %get-tuple-element.61.g1_ref, ...), custom_call_target="tpu_custom_call" | custom-call | flops 2293760000 | bytes 12615680 | tf_op jit(solution)/shard_map/adamw/pallas_call | solution.py:447
  268.8 1.1 collective-permute-start.18
  270.9 6.7 %adamw.4 = (bf16[2,112,2560]{2,1,0:T(8,128)(2,1)}, f32[2,112,2560]{2,1,0:T(8,128)}, f32[2,112,2560]{2,1,0:T(8,128)}) custom-call(s32[1]{0:T(128)} %bitcast.me_ref, f32[8,128]{1,0:T(8,128)} %get-tuple-element.53.squares_ref, bf16[112,2560]{1,0:T(8,128)(2,1)} %get-tuple-element.57.g0_ref, bf16[112,2560]{1,0:T(8,128)(2,1)} %get-tuple-element.58.g1_ref, ...), custom_call_target="tpu_custom_call" | custom-call | flops 2293760000 | bytes 12615680 | tf_op jit(solution)/shard_map/adamw/pallas_call | solution.py:447
  277.5 1.2 collective-permute-start.9
  278.7 6.8 %adamw.3 = (bf16[2,112,2560]{2,1,0:T(8,128)(2,1)}, f32[2,112,2560]{2,1,0:T(8,128)}, f32[2,112,2560]{2,1,0:T(8,128)}) custom-call(s32[1]{0:T(128)} %bitcast.me_ref, f32[8,128]{1,0:T(8,128)} %get-tuple-element.53.squares_ref, bf16[112,2560]{1,0:T(8,128)(2,1)} %get-tuple-element.54.g0_ref, bf16[112,2560]{1,0:T(8,128)(2,1)} %get-tuple-element.55.g1_ref, ...), custom_call_target="tpu_custom_call" | custom-call | flops 2293760000 | bytes 12615680 | tf_op jit(solution)/shard_map/adamw/pallas_call | solution.py:447
  286.4 10.9 %collective-permute-done.18.refs_2_ = bf16[2,320,896]{2,1,0:T(8,128)(2,1)} collective-permute-done((bf16[2,320,896]{2,1,0:T(8,128)(2,1)}, bf16[2,320,896]{2,1,0:T(8,128)(2,1)}, u32[]{:S(2)}, u32[]{:S(2)}) %collective-permute-start.18) | collective-permute-done | bytes 1146912 | tf_op jit(solution)/shard_map/ppermute | solution.py:426
  297.3 1.2 collective-permute-start.12
  299.4 22.5 %collective-permute-done.9.refs_2_ = bf16[2,112,2560]{2,1,0:T(8,128)(2,1)} collective-permute-done((bf16[2,112,2560]{2,1,0:T(8,128)(2,1)}, bf16[2,112,2560]{2,1,0:T(8,128)(2,1)}, u32[]{:S(2)}, u32[]{:S(2)}) %collective-permute-start.9) | collective-permute-done | bytes 1146912 | tf_op jit(solution)/shard_map/ppermute | solution.py:426
  322.9 22.7 %collective-permute-done.refs_2_ = bf16[2,112,2560]{2,1,0:T(8,128)(2,1)} collective-permute-done((bf16[2,112,2560]{2,1,0:T(8,128)(2,1)}, bf16[2,112,2560]{2,1,0:T(8,128)(2,1)}, u32[]{:S(2)}, u32[]{:S(2)}) %collective-permute-start) | collective-permute-done | bytes 1146912 | tf_op jit(solution)/shard_map/ppermute | solution.py:426
  345.6 1.1 collective-permute-start.10
  348.7 1.1 slice.28
  349.9 1.1 collective-permute-start.19
  351.0 1.1 slice.27
  353.1 6.6 %collective-permute-done.10.refs_0_ = bf16[2,48,2560]{2,1,0:T(8,128)(2,1)S(1)} collective-permute-done((bf16[2,48,2560]{2,1,0:T(8,128)(2,1)S(1)}, bf16[2,48,2560]{2,1,0:T(8,128)(2,1)S(1)}, u32[]{:S(2)}, u32[]{:S(2)}) %collective-permute-start.10) | collective-permute-done | bytes 491552 | tf_op jit(solution)/shard_map/ppermute | solution.py:426
  360.5 1.1 slice.29
  361.6 8.6 %collective-permute-done.1.refs_0_ = bf16[2,48,2560]{2,1,0:T(8,128)(2,1)S(1)} collective-permute-done((bf16[2,48,2560]{2,1,0:T(8,128)(2,1)S(1)}, bf16[2,48,2560]{2,1,0:T(8,128)(2,1)S(1)}, u32[]{:S(2)}, u32[]{:S(2)}) %collective-permute-start.1) | collective-permute-done | bytes 491552 | tf_op jit(solution)/shard_map/ppermute | solution.py:426
  371.1 1.1 collective-permute-start.22
  372.1 1.1 slice.25
  373.3 7.8 %collective-permute-done.19.refs_0_ = bf16[2,160,896]{2,1,0:T(8,128)(2,1)S(1)} collective-permute-done((bf16[2,160,896]{2,1,0:T(8,128)(2,1)S(1)}, bf16[2,160,896]{2,1,0:T(8,128)(2,1)S(1)}, u32[]{:S(2)}, u32[]{:S(2)}) %collective-permute-start.19) | collective-permute-done | bytes 573472 | tf_op jit(solution)/shard_map/ppermute | solution.py:426
  382.1 1.8 collective-permute-done.22.refs_2_
  384.4 12.8 %collective-permute-done.4.refs_2_ = bf16[2,64,2560]{2,1,0:T(8,128)(2,1)} collective-permute-done((bf16[2,64,2560]{2,1,0:T(8,128)(2,1)S(1)}, bf16[2,64,2560]{2,1,0:T(8,128)(2,1)}, u32[]{:S(2)}, u32[]{:S(2)}) %collective-permute-start.4) | collective-permute-done | bytes 655392 | tf_op jit(solution)/shard_map/ppermute | solution.py:426
  397.8 1.4 collective-permute-done.20.refs_1_
  400.2 5.8 %place.10.refs_4_ = bf16[2,8,320,896]{3,2,1,0:T(8,128)(2,1)} custom-call(bf16[2,320,896]{2,1,0:T(8,128)(2,1)} %get-tuple-element.62.refs_0_, bf16[2,320,896]{2,1,0:T(8,128)(2,1)} %collective-permute-done.24.refs_1_, bf16[2,320,896]{2,1,0:T(8,128)(2,1)} %collective-permute-done.18.refs_2_, bf16[2,320,896]{2,1,0:T(8,128)(2,1)} %collective-permute-done.25.refs_3_, ...), custom_call_target="tpu_custom_call" | custom-call | flops 4128768000 | bytes 13762560 | tf_op jit(solution)/shard_map/place/pallas_call | solution.py:496
  406.5 5.8 %place.8.refs_4_ = bf16[2,8,112,2560]{3,2,1,0:T(8,128)(2,1)} custom-call(bf16[2,112,2560]{2,1,0:T(8,128)(2,1)} %get-tuple-element.59.refs_0_, bf16[2,112,2560]{2,1,0:T(8,128)(2,1)} %collective-permute-done.15.refs_1_, bf16[2,112,2560]{2,1,0:T(8,128)(2,1)} %collective-permute-done.9.refs_2_, bf16[2,112,2560]{2,1,0:T(8,128)(2,1)} %collective-permute-done.16.refs_3_, ...), custom_call_target="tpu_custom_call" | custom-call | flops 4128768000 | bytes 13762560 | tf_op jit(solution)/shard_map/place/pallas_call | solution.py:496
  412.7 2.5 place.11
  415.3 5.8 %place.6.refs_4_ = bf16[2,8,112,2560]{3,2,1,0:T(8,128)(2,1)} custom-call(bf16[2,112,2560]{2,1,0:T(8,128)(2,1)} %get-tuple-element.56.refs_0_, bf16[2,112,2560]{2,1,0:T(8,128)(2,1)} %collective-permute-done.6.refs_1_, bf16[2,112,2560]{2,1,0:T(8,128)(2,1)} %collective-permute-done.refs_2_, bf16[2,112,2560]{2,1,0:T(8,128)(2,1)} %collective-permute-done.7.refs_3_, ...), custom_call_target="tpu_custom_call" | custom-call | flops 4128768000 | bytes 13762560 | tf_op jit(solution)/shard_map/place/pallas_call | solution.py:496
  421.1 2.6 place.9
  423.7 2.6 place.7
  (49 shorter events, 12.7 us)
Async XLA Ops:
  268.8 28.5 %collective-permute-start.18 = (bf16[2,320,896]{2,1,0:T(8,128)(2,1)}, bf16[2,320,896]{2,1,0:T(8,128)(2,1)}, u32[]{:S(2)}, u32[]{:S(2)}) collective-permute-start(bf16[2,320,896]{2,1,0:T(8,128)(2,1)} %get-tuple-element.62.refs_0_), channel_id=1, source_target_pairs={{0,4},{1,5},{2,6},{3,7},{4,0},{5,1},{6,2},{7,3}} | collective-permute-start | bytes 3440648 | tf_op jit(solution)/shard_map/ppermute | solution.py:426
  269.9 28.5 %collective-permute-start.21 = (bf16[2,320,896]{2,1,0:T(8,128)(2,1)}, bf16[2,320,896]{2,1,0:T(8,128)(2,1)}, u32[]{:S(2)}, u32[]{:S(2)}) collective-permute-start(bf16[2,320,896]{2,1,0:T(8,128)(2,1)} %get-tuple-element.62.refs_0_), channel_id=1, source_target_pairs={{0,2},{1,3},{2,0},{3,1},{4,6},{5,7},{6,4},{7,5}} | collective-permute-start | bytes 3440648 | tf_op jit(solution)/shard_map/ppermute | solution.py:426
  270.8 27.6 %collective-permute-start.24 = (bf16[2,320,896]{2,1,0:T(8,128)(2,1)}, bf16[2,320,896]{2,1,0:T(8,128)(2,1)}, u32[]{:S(2)}, u32[]{:S(2)}) collective-permute-start(bf16[2,320,896]{2,1,0:T(8,128)(2,1)} %get-tuple-element.62.refs_0_), channel_id=1, source_target_pairs={{0,1},{1,0},{2,3},{3,2},{4,5},{5,4},{6,7},{7,6}} | collective-permute-start | bytes 3440648 | tf_op jit(solution)/shard_map/ppermute | solution.py:426
  277.5 44.3 %collective-permute-start.9 = (bf16[2,112,2560]{2,1,0:T(8,128)(2,1)}, bf16[2,112,2560]{2,1,0:T(8,128)(2,1)}, u32[]{:S(2)}, u32[]{:S(2)}) collective-permute-start(bf16[2,112,2560]{2,1,0:T(8,128)(2,1)} %get-tuple-element.59.refs_0_), channel_id=1, source_target_pairs={{0,4},{1,5},{2,6},{3,7},{4,0},{5,1},{6,2},{7,3}} | collective-permute-start | bytes 3440648 | tf_op jit(solution)/shard_map/ppermute | solution.py:426
  285.5 60.2 %collective-permute-start = (bf16[2,112,2560]{2,1,0:T(8,128)(2,1)}, bf16[2,112,2560]{2,1,0:T(8,128)(2,1)}, u32[]{:S(2)}, u32[]{:S(2)}) collective-permute-start(bf16[2,112,2560]{2,1,0:T(8,128)(2,1)} %get-tuple-element.56.refs_0_), channel_id=1, source_target_pairs={{0,4},{1,5},{2,6},{3,7},{4,0},{5,1},{6,2},{7,3}} | collective-permute-start | bytes 3440648 | tf_op jit(solution)/shard_map/ppermute | solution.py:426
  297.3 50.5 %collective-permute-start.12 = (bf16[2,112,2560]{2,1,0:T(8,128)(2,1)}, bf16[2,112,2560]{2,1,0:T(8,128)(2,1)}, u32[]{:S(2)}, u32[]{:S(2)}) collective-permute-start(bf16[2,112,2560]{2,1,0:T(8,128)(2,1)} %get-tuple-element.59.refs_0_), channel_id=1, source_target_pairs={{0,2},{1,3},{2,0},{3,1},{4,6},{5,7},{6,4},{7,5}} | collective-permute-start | bytes 3440648 | tf_op jit(solution)/shard_map/ppermute | solution.py:426
  298.4 51.4 %collective-permute-start.15 = (bf16[2,112,2560]{2,1,0:T(8,128)(2,1)}, bf16[2,112,2560]{2,1,0:T(8,128)(2,1)}, u32[]{:S(2)}, u32[]{:S(2)}) collective-permute-start(bf16[2,112,2560]{2,1,0:T(8,128)(2,1)} %get-tuple-element.59.refs_0_), channel_id=1, source_target_pairs={{0,1},{1,0},{2,3},{3,2},{4,5},{5,4},{6,7},{7,6}} | collective-permute-start | bytes 3440648 | tf_op jit(solution)/shard_map/ppermute | solution.py:426
  298.5 53.6 %collective-permute-start.3 = (bf16[2,112,2560]{2,1,0:T(8,128)(2,1)}, bf16[2,112,2560]{2,1,0:T(8,128)(2,1)}, u32[]{:S(2)}, u32[]{:S(2)}) collective-permute-start(bf16[2,112,2560]{2,1,0:T(8,128)(2,1)} %get-tuple-element.56.refs_0_), channel_id=1, source_target_pairs={{0,2},{1,3},{2,0},{3,1},{4,6},{5,7},{6,4},{7,5}} | collective-permute-start | bytes 3440648 | tf_op jit(solution)/shard_map/ppermute | solution.py:426
  321.9 31.3 %collective-permute-start.6 = (bf16[2,112,2560]{2,1,0:T(8,128)(2,1)}, bf16[2,112,2560]{2,1,0:T(8,128)(2,1)}, u32[]{:S(2)}, u32[]{:S(2)}) collective-permute-start(bf16[2,112,2560]{2,1,0:T(8,128)(2,1)} %get-tuple-element.56.refs_0_), channel_id=1, source_target_pairs={{0,1},{1,0},{2,3},{3,2},{4,5},{5,4},{6,7},{7,6}} | collective-permute-start | bytes 3440648 | tf_op jit(solution)/shard_map/ppermute | solution.py:426
  345.6 14.1 %collective-permute-start.10 = (bf16[2,48,2560]{2,1,0:T(8,128)(2,1)S(1)}, bf16[2,48,2560]{2,1,0:T(8,128)(2,1)S(1)}, u32[]{:S(2)}, u32[]{:S(2)}) collective-permute-start(bf16[2,48,2560]{2,1,0:T(8,128)(2,1)S(1)} %slice.26), channel_id=1, source_target_pairs={{0,2},{1,3},{2,0},{3,1},{4,6},{5,7},{6,4},{7,5}} | collective-permute-start | bytes 1474568 | tf_op jit(solution)/shard_map/ppermute | solution.py:426
  347.8 22.5 %collective-permute-start.1 = (bf16[2,48,2560]{2,1,0:T(8,128)(2,1)S(1)}, bf16[2,48,2560]{2,1,0:T(8,128)(2,1)S(1)}, u32[]{:S(2)}, u32[]{:S(2)}) collective-permute-start(bf16[2,48,2560]{2,1,0:T(8,128)(2,1)S(1)} %slice.24), channel_id=1, source_target_pairs={{0,2},{1,3},{2,0},{3,1},{4,6},{5,7},{6,4},{7,5}} | collective-permute-start | bytes 1474568 | tf_op jit(solution)/shard_map/ppermute | solution.py:426
  349.9 31.2 %collective-permute-start.19 = (bf16[2,160,896]{2,1,0:T(8,128)(2,1)S(1)}, bf16[2,160,896]{2,1,0:T(8,128)(2,1)S(1)}, u32[]{:S(2)}, u32[]{:S(2)}) collective-permute-start(bf16[2,160,896]{2,1,0:T(8,128)(2,1)S(1)} %slice.28), channel_id=1, source_target_pairs={{0,2},{1,3},{2,0},{3,1},{4,6},{5,7},{6,4},{7,5}} | collective-permute-start | bytes 1720328 | tf_op jit(solution)/shard_map/ppermute | solution.py:426
  352.1 31.8 %collective-permute-start.13 = (bf16[2,64,2560]{2,1,0:T(8,128)(2,1)S(1)}, bf16[2,64,2560]{2,1,0:T(8,128)(2,1)}, u32[]{:S(2)}, u32[]{:S(2)}) collective-permute-start(bf16[2,64,2560]{2,1,0:T(8,128)(2,1)S(1)} %slice.27), channel_id=1, source_target_pairs={{0,4},{1,5},{2,6},{3,7},{4,0},{5,1},{6,2},{7,3}} | collective-permute-start | bytes 1966088 | tf_op jit(solution)/shard_map/ppermute | solution.py:426
  353.1 44.1 %collective-permute-start.25 = (bf16[2,320,896]{2,1,0:T(8,128)(2,1)}, bf16[2,320,896]{2,1,0:T(8,128)(2,1)}, u32[]{:S(2)}, u32[]{:S(2)}) collective-permute-start(bf16[2,320,896]{2,1,0:T(8,128)(2,1)} %collective-permute-done.18.refs_2_), channel_id=1, source_target_pairs={{0,1},{1,0},{2,3},{3,2},{4,5},{5,4},{6,7},{7,6}} | collective-permute-start | bytes 3440648 | tf_op jit(solution)/shard_map/ppermute | solution.py:426
  359.7 0.8 copy-start.3
  360.5 37.2 %collective-permute-start.26 = (bf16[2,320,896]{2,1,0:T(8,128)(2,1)}, bf16[2,320,896]{2,1,0:T(8,128)(2,1)}, u32[]{:S(2)}, u32[]{:S(2)}) collective-permute-start(bf16[2,320,896]{2,1,0:T(8,128)(2,1)} %collective-permute-done.21.refs_4_), channel_id=1, source_target_pairs={{0,1},{1,0},{2,3},{3,2},{4,5},{5,4},{6,7},{7,6}} | collective-permute-start | bytes 3440648 | tf_op jit(solution)/shard_map/ppermute | solution.py:426
  370.2 0.8 copy-start.2
  371.1 12.8 %collective-permute-start.22 = (bf16[2,160,896]{2,1,0:T(8,128)(2,1)S(1)}, bf16[2,160,896]{2,1,0:T(8,128)(2,1)}, u32[]{:S(2)}, u32[]{:S(2)}) collective-permute-start(bf16[2,160,896]{2,1,0:T(8,128)(2,1)S(1)} %slice.29), channel_id=1, source_target_pairs={{0,4},{1,5},{2,6},{3,7},{4,0},{5,1},{6,2},{7,3}} | collective-permute-start | bytes 1720328 | tf_op jit(solution)/shard_map/ppermute | solution.py:426
  381.1 16.2 %copy-start = (bf16[2,160,896]{2,1,0:T(8,128)(2,1)}, bf16[2,160,896]{2,1,0:T(8,128)(2,1)S(1)}, u32[]{:S(2)}) copy-start(bf16[2,160,896]{2,1,0:T(8,128)(2,1)S(1)} %collective-permute-done.19.refs_0_) | copy-start | bytes 1720324
  381.1 16.2 %collective-permute-start.4 = (bf16[2,64,2560]{2,1,0:T(8,128)(2,1)S(1)}, bf16[2,64,2560]{2,1,0:T(8,128)(2,1)}, u32[]{:S(2)}, u32[]{:S(2)}) collective-permute-start(bf16[2,64,2560]{2,1,0:T(8,128)(2,1)S(1)} %slice.25), channel_id=1, source_target_pairs={{0,4},{1,5},{2,6},{3,7},{4,0},{5,1},{6,2},{7,3}} | collective-permute-start | bytes 1966088 | tf_op jit(solution)/shard_map/ppermute | solution.py:426
  383.9 22.1 %collective-permute-start.16 = (bf16[2,112,2560]{2,1,0:T(8,128)(2,1)}, bf16[2,112,2560]{2,1,0:T(8,128)(2,1)}, u32[]{:S(2)}, u32[]{:S(2)}) collective-permute-start(bf16[2,112,2560]{2,1,0:T(8,128)(2,1)} %collective-permute-done.9.refs_2_), channel_id=1, source_target_pairs={{0,1},{1,0},{2,3},{3,2},{4,5},{5,4},{6,7},{7,6}} | collective-permute-start | bytes 3440648 | tf_op jit(solution)/shard_map/ppermute | solution.py:426
  383.9 22.5 %collective-permute-start.17 = (bf16[2,112,2560]{2,1,0:T(8,128)(2,1)}, bf16[2,112,2560]{2,1,0:T(8,128)(2,1)}, u32[]{:S(2)}, u32[]{:S(2)}) collective-permute-start(bf16[2,112,2560]{2,1,0:T(8,128)(2,1)} %collective-permute-done.12.refs_4_), channel_id=1, source_target_pairs={{0,1},{1,0},{2,3},{3,2},{4,5},{5,4},{6,7},{7,6}} | collective-permute-start | bytes 3440648 | tf_op jit(solution)/shard_map/ppermute | solution.py:426
  397.2 2.0 collective-permute-start.20
  397.2 17.9 %collective-permute-start.7 = (bf16[2,112,2560]{2,1,0:T(8,128)(2,1)}, bf16[2,112,2560]{2,1,0:T(8,128)(2,1)}, u32[]{:S(2)}, u32[]{:S(2)}) collective-permute-start(bf16[2,112,2560]{2,1,0:T(8,128)(2,1)} %collective-permute-done.refs_2_), channel_id=1, source_target_pairs={{0,1},{1,0},{2,3},{3,2},{4,5},{5,4},{6,7},{7,6}} | collective-permute-start | bytes 3440648 | tf_op jit(solution)/shard_map/ppermute | solution.py:426
  397.8 17.6 %collective-permute-start.8 = (bf16[2,112,2560]{2,1,0:T(8,128)(2,1)}, bf16[2,112,2560]{2,1,0:T(8,128)(2,1)}, u32[]{:S(2)}, u32[]{:S(2)}) collective-permute-start(bf16[2,112,2560]{2,1,0:T(8,128)(2,1)} %collective-permute-done.3.refs_4_), channel_id=1, source_target_pairs={{0,1},{1,0},{2,3},{3,2},{4,5},{5,4},{6,7},{7,6}} | collective-permute-start | bytes 3440648 | tf_op jit(solution)/shard_map/ppermute | solution.py:426
  399.2 0.8 copy-start.1
  400.1 12.2 %collective-permute-start.23 = (bf16[2,160,896]{2,1,0:T(8,128)(2,1)}, bf16[2,160,896]{2,1,0:T(8,128)(2,1)}, u32[]{:S(2)}, u32[]{:S(2)}) collective-permute-start(bf16[2,160,896]{2,1,0:T(8,128)(2,1)} %collective-permute-done.22.refs_2_), channel_id=1, source_target_pairs={{0,1},{1,0},{2,3},{3,2},{4,5},{5,4},{6,7},{7,6}} | collective-permute-start | bytes 1720328 | tf_op jit(solution)/shard_map/ppermute | solution.py:426
  406.0 15.1 %collective-permute-start.14 = (bf16[2,64,2560]{2,1,0:T(8,128)(2,1)}, bf16[2,64,2560]{2,1,0:T(8,128)(2,1)}, u32[]{:S(2)}, u32[]{:S(2)}) collective-permute-start(bf16[2,64,2560]{2,1,0:T(8,128)(2,1)} %collective-permute-done.13.refs_2_), channel_id=1, source_target_pairs={{0,1},{1,0},{2,3},{3,2},{4,5},{5,4},{6,7},{7,6}} | collective-permute-start | bytes 1966088 | tf_op jit(solution)/shard_map/ppermute | solution.py:426
  406.4 17.4 %collective-permute-start.5 = (bf16[2,64,2560]{2,1,0:T(8,128)(2,1)}, bf16[2,64,2560]{2,1,0:T(8,128)(2,1)}, u32[]{:S(2)}, u32[]{:S(2)}) collective-permute-start(bf16[2,64,2560]{2,1,0:T(8,128)(2,1)} %collective-permute-done.4.refs_2_), channel_id=1, source_target_pairs={{0,1},{1,0},{2,3},{3,2},{4,5},{5,4},{6,7},{7,6}} | collective-permute-start | bytes 1966088 | tf_op jit(solution)/shard_map/ppermute | solution.py:426
  412.3 8.8 %collective-permute-start.11 = (bf16[2,48,2560]{2,1,0:T(8,128)(2,1)}, bf16[2,48,2560]{2,1,0:T(8,128)(2,1)}, u32[]{:S(2)}, u32[]{:S(2)}) collective-permute-start(bf16[2,48,2560]{2,1,0:T(8,128)(2,1)} %copy-done.3), channel_id=1, source_target_pairs={{0,1},{1,0},{2,3},{3,2},{4,5},{5,4},{6,7},{7,6}} | collective-permute-start | bytes 1474568 | tf_op jit(solution)/shard_map/ppermute | solution.py:426
  415.1 8.6 %collective-permute-start.2 = (bf16[2,48,2560]{2,1,0:T(8,128)(2,1)}, bf16[2,48,2560]{2,1,0:T(8,128)(2,1)}, u32[]{:S(2)}, u32[]{:S(2)}) collective-permute-start(bf16[2,48,2560]{2,1,0:T(8,128)(2,1)} %copy-done.2), channel_id=1, source_target_pairs={{0,1},{1,0},{2,3},{3,2},{4,5},{5,4},{6,7},{7,6}} | collective-permute-start | bytes 1474568 | tf_op jit(solution)/shard_map/ppermute | solution.py:426
